TPU v7x, 64 devices: a 2x2x8 block of a 4x4x8 slice. The times are simulated.
64 devices in a mesh: cfg: 4 (over x, y), cp: 16 (over z, core).
Axes of the slice: x: 2, y: 2, z: 8, core: 2. Of those that a mesh axis runs over, the one named last changes fastest.
The devices are a block of a 4x4x8 slice.
Arguments:
- video_states: bfloat16 [4, 3072, 1920], P('cfg', 'cp'), parts along dimension 0
- text_states: bfloat16 [4, 226, 1920], P('cfg'), parts along dimension 0
- time_emb: float32 [4, 512], P('cfg'), parts along dimension 0
- rope_angle: float32 [3072, 32], P('cp')
- ada1_w: bfloat16 [512, 11520], replicated
- ada1_b: float32 [11520], replicated
- norm1_par: float32 [2, 1920], replicated
- w_qkv: bfloat16 [1920, 5760], replicated
- b_qkv: float32 [5760], replicated
- qk_norm: float32 [4, 64], replicated
- w_out: bfloat16 [1920, 1920], replicated
- b_out: float32 [1920], replicated
- ada2_w: bfloat16 [512, 11520], replicated
- ada2_b: float32 [11520], replicated
- norm2_par: float32 [2, 1920], replicated
- w_up: bfloat16 [1920, 7680], replicated
- b_up: float32 [7680], replicated
- w_down: bfloat16 [7680, 1920], replicated
- b_down: float32 [1920], replicated
Outputs:
- output 1: bfloat16 [4, 3072, 1920], P('cfg', 'cp'), parts along dimension 0
- output 2: bfloat16 [4, 226, 1920], P('cfg'), parts along dimension 0
There are 4 independent parts. A program takes and returns all parts, laid end to end along the dimension named above; an argument that names none is the same for every part.
All inputs are finite; a program needn't handle non-finite values.
Results may differ from a plain program's by a relative error of at most 0.00948666.
Values are sent between devices in bfloat16 or wider.
A program may use at most 768 MiB of HBM per device.

v0:
```python
import jax
import jax.numpy as jnp
from jax import lax
from jax.sharding import PartitionSpec as P

LN_EPS = 1e-5
QK_EPS = 1e-6


def layer_norm(values, gain_vec, bias_vec, epsilon):
    mean_val = jnp.mean(values, axis=-1, keepdims=True)
    centred = values - mean_val
    var_val = jnp.mean(centred * centred, axis=-1, keepdims=True)
    return centred * lax.rsqrt(var_val + epsilon) * gain_vec + bias_vec


def modulation(time_emb, ada_w, ada_b):
    silu_in = jax.nn.silu(time_emb).astype(jnp.bfloat16)
    emb_all = jnp.dot(silu_in, ada_w, preferred_element_type=jnp.float32) + ada_b
    return jnp.split(emb_all, 6, axis=-1)


def ada_norm(states, norm_par, shift_row, scale_row):
    normed = layer_norm(states.astype(jnp.float32), norm_par[0], norm_par[1], LN_EPS)
    return (normed * (1.0 + scale_row) + shift_row).astype(jnp.bfloat16)


def rotate(values, angles):
    cos_a = jnp.cos(angles)[:, None, :]
    sin_a = jnp.sin(angles)[:, None, :]
    pair_view = values.reshape(values.shape[:-1] + (-1, 2))
    even_part = pair_view[..., 0]
    odd_part = pair_view[..., 1]
    rotated = jnp.stack([even_part * cos_a - odd_part * sin_a, odd_part * cos_a + even_part * sin_a], axis=-1)
    return rotated.reshape(values.shape)


def project_qkv(tokens, rope_angle, w_qkv, b_qkv, qk_norm, n_text):
    head_dim = qk_norm.shape[-1]
    head_shape = (tokens.shape[0], tokens.shape[1] // head_dim, head_dim)
    qkv_all = jnp.dot(tokens, w_qkv, preferred_element_type=jnp.float32) + b_qkv
    q_raw, k_raw, v_raw = jnp.split(qkv_all, 3, axis=-1)
    q_heads = layer_norm(q_raw.reshape(head_shape), qk_norm[0], qk_norm[1], QK_EPS)
    k_heads = layer_norm(k_raw.reshape(head_shape), qk_norm[2], qk_norm[3], QK_EPS)
    q_heads = jnp.concatenate([q_heads[:n_text], rotate(q_heads[n_text:], rope_angle)], axis=0)
    k_heads = jnp.concatenate([k_heads[:n_text], rotate(k_heads[n_text:], rope_angle)], axis=0)
    return q_heads.astype(jnp.bfloat16), k_heads.astype(jnp.bfloat16), v_raw.reshape(head_shape).astype(jnp.bfloat16)


def attend_update(att_state, queries, key_blk, val_blk):
    run_max, run_sum, run_acc = att_state
    qk_scale = queries.shape[-1] ** -0.5
    scores = jnp.einsum('qhd,khd->hqk', queries, key_blk, preferred_element_type=jnp.float32) * qk_scale
    new_max = jnp.maximum(run_max, jnp.max(scores, axis=-1))
    rescale = jnp.exp(run_max - new_max)
    attn_prob = jnp.exp(scores - new_max[..., None])
    new_sum = run_sum * rescale + jnp.sum(attn_prob, axis=-1)
    new_acc = run_acc * rescale[..., None] + jnp.einsum('hqk,khd->hqd', attn_prob.astype(jnp.bfloat16), val_blk, preferred_element_type=jnp.float32)
    return new_max, new_sum, new_acc


def block_tail(vid_in, txt_in, attn_proj, vid_gate, txt_gate, time_emb, ada2_w, ada2_b, norm2_par, w_up, b_up, w_down, b_down):
    n_text = txt_in.shape[0]
    txt_mid = (txt_in.astype(jnp.float32) + txt_gate * attn_proj[:n_text]).astype(jnp.bfloat16)
    vid_mid = (vid_in.astype(jnp.float32) + vid_gate * attn_proj[n_text:]).astype(jnp.bfloat16)
    vid_shift, vid_scale, vid_gate2, txt_shift, txt_scale, txt_gate2 = modulation(time_emb, ada2_w, ada2_b)
    tokens = jnp.concatenate([ada_norm(txt_mid, norm2_par, txt_shift, txt_scale), ada_norm(vid_mid, norm2_par, vid_shift, vid_scale)], axis=0)
    up_proj = jnp.dot(tokens, w_up, preferred_element_type=jnp.float32) + b_up
    gelu_out = jax.nn.gelu(up_proj, approximate=True).astype(jnp.bfloat16)
    ffn_out = jnp.dot(gelu_out, w_down, preferred_element_type=jnp.float32) + b_down
    txt_out = (txt_mid.astype(jnp.float32) + txt_gate2 * ffn_out[:n_text]).astype(jnp.bfloat16)
    vid_out = (vid_mid.astype(jnp.float32) + vid_gate2 * ffn_out[n_text:]).astype(jnp.bfloat16)
    return vid_out, txt_out


def solution(mesh):
    cp_size = mesh.shape['cp']
    shift_pairs = [(rank_idx, (rank_idx + 1) % cp_size) for rank_idx in range(cp_size)]

    def device_block(video_states, text_states, time_emb, rope_angle, ada1_w, ada1_b, norm1_par, w_qkv, b_qkv, qk_norm, w_out, b_out, ada2_w, ada2_b, norm2_par, w_up, b_up, w_down, b_down):
        vid_in = video_states[0]
        txt_in = text_states[0]
        n_text = txt_in.shape[0]
        vid_shift, vid_scale, vid_gate, txt_shift, txt_scale, txt_gate = modulation(time_emb, ada1_w, ada1_b)
        tokens = jnp.concatenate([ada_norm(txt_in, norm1_par, txt_shift, txt_scale), ada_norm(vid_in, norm1_par, vid_shift, vid_scale)], axis=0)
        queries, key_loc, val_loc = project_qkv(tokens, rope_angle, w_qkv, b_qkv, qk_norm, n_text)
        n_rows, n_heads, head_dim = queries.shape
        init_state = (jnp.full((n_heads, n_rows), -jnp.inf, jnp.float32), jnp.zeros((n_heads, n_rows), jnp.float32), jnp.zeros((n_heads, n_rows, head_dim), jnp.float32))
        first_state = attend_update(init_state, queries, key_loc, val_loc)

        def pass_step(step_idx, loop_state):
            att_state, kv_blk = loop_state
            kv_blk = lax.ppermute(kv_blk, 'cp', shift_pairs)
            return attend_update(att_state, queries, kv_blk[0], kv_blk[1]), kv_blk

        final_state = lax.fori_loop(0, cp_size - 1, pass_step, (first_state, (key_loc[n_text:], val_loc[n_text:])))[0]
        att_out = (final_state[2] / final_state[1][..., None]).astype(jnp.bfloat16)
        w_out_heads = w_out.reshape(n_heads, head_dim, w_out.shape[-1])
        attn_proj = jnp.einsum('hqd,hde->qe', att_out, w_out_heads, preferred_element_type=jnp.float32) + b_out
        vid_out, txt_out = block_tail(vid_in, txt_in, attn_proj, vid_gate, txt_gate, time_emb, ada2_w, ada2_b, norm2_par, w_up, b_up, w_down, b_down)
        return vid_out[None], txt_out[None]

    in_specs = (P('cfg', 'cp', None), P('cfg', None, None), P('cfg', None), P('cp', None)) + (P(),) * 15
    out_specs = (P('cfg', 'cp', None), P('cfg', None, None))
    return jax.shard_map(device_block, mesh=mesh, in_specs=in_specs, out_specs=out_specs, check_vma=False)
```

profile of v0, /device:TPU:30, one launch (start us, length us, event | category | flops | bytes accessed | tf_op | source)
XLA Modules:
  0.0 717.5 jit_solution(6591711420139433004)
XLA Ops:
  17.5 18.7 %fusion.111 = (bf16[418,5760]{1,0:T(8,128)(2,1)}, f32[418,5760]{1,0:T(8,128)}) fusion(f32[5760]{0:T(1024)S(1)} %copy-done.30, bf16[1920,5760]{1,0:T(8,128)(2,1)} %param.28, bf16[192,1920]{1,0:T(8,128)(2,1)S(1)} %fusion.84, bf16[226,1920]{1,0:T(8,128)(2,1)S(1)} %fusion.57), kind=kOutput, calls=%fused_computation.173 | convolution fusion | flops 9253516288 | bytes 38192640 | tf_op jit(solution)/shard_map/dot_general | solution.py:41
  90.6 8.2 %subtract_convert_fusion.1 = (bf16[192,30,32,1]{0,3,2,1:T(2,128)(2,1)S(1)}, bf16[192,30,32,1]{0,3,2,1:T(2,128)(2,1)S(1)}, bf16[192,30,32,1]{0,3,2,1:T(2,128)(2,1)S(1)}, bf16[192,30,32,1]{0,3,2,1:T(2,128)(2,1)}) fusion(f32[192,30,32,2]{0,3,2,1:T(2,128)} %reshape.132, f32[192,32]{0,1:T(8,128)S(1)} %get-tuple-element.98, f32[192,32]{0,1:T(8,128)S(1)} %get-tuple-element.97, ...), kind=kLoop, calls=%fused_computation.117 | loop fusion | flops 2949120 | bytes 4472832 | tf_op jit(solution)/shard_map/convert.10
  114.2 10.7 %multiply_reduce_fusion.1 = (f32[30,418]{1,0:T(8,128)S(1)}, f32[30,418,418]{1,2,0:T(8,128)}) fusion(bf16[192,30,64]{0,2,1:T(8,128)(2,1)S(1)} %reshape.136, bf16[226,30,64]{0,2,1:T(8,128)(2,1)S(1)} %copy-done.11, bf16[192,30,64]{0,2,1:T(8,128)(2,1)S(1)} %reshape.133, bf16[226,30,64]{0,2,1:T(8,128)(2,1)S(1)} %copy-done.9), kind=kOutput, calls=%fused_computation.12 | convolution fusion | flops 687831552 | bytes 24227280 | tf_op jit(solution)/shard_map/qhd,khd->hqk/dot_general | solution.py:53
  124.9 11.1 %fusion.10 = f32[30,418]{1,0:T(8,128)S(1)} fusion(f32[30,418,418]{1,2,0:T(8,128)} %get-tuple-element.104, f32[30,418]{1,0:T(8,128)S(1)} %get-tuple-element.163), kind=kLoop, calls=%fused_computation.14 | loop fusion | flops 15712620 | bytes 21067200 | tf_op jit(solution)/shard_map/reduce_sum | solution.py:57
  136.1 12.7 %fusion.36 = f32[30,418,64]{1,2,0:T(8,128)} fusion(bf16[418,30,64]{0,2,1:T(8,128)(2,1)S(1)} %bitcast.111, f32[30,418,418]{1,2,0:T(8,128)} %get-tuple-element.104, f32[30,418]{1,0:T(8,128)S(1)} %get-tuple-element.163, f32[30,418]{1,0:T(8,128)S(1)} %get-tuple-element.93), kind=kOutput, calls=%fused_computation.55 | convolution fusion | flops 687467904 | bytes 25882560 | tf_op jit(solution)/shard_map/hqk,khd->hqd/dot_general | solution.py:58
  148.7 512.4 %while.18 = (s32[]{:T(128)}, f32[30,418]{1,0:T(8,128)S(1)}, f32[30,418]{1,0:T(8,128)S(1)}, f32[30,418,64]{1,2,0:T(8,128)}, bf16[192,30,64]{0,2,1:T(8,128)(2,1)S(...) while((s32[]{:T(128)}, f32[30,418]{1,0:T(8,128)S(1)}, ...), condition=%wide.region_13.14_spmd, body=%wide.region_10.13_spmd.sunk | while | flops 637257728 | bytes 112247296 | solution.py:96
  151.2 16.3 %collective-permute-done = bf16[192,30,64]{0,2,1:T(8,128)(2,1)S(1)} collective-permute-done((bf16[192,30,64]{0,2,1:T(8,128)(2,1)S(1)}, bf16[192,30,64]{0,2,1:T(8,128)(2,1)S(1)}, u32[]{:S(2)}, u32[]{:S(2)}) %collective-permute-start) | collective-permute-done | bytes 737312 | tf_op jit(solution)/shard_map/while/body/eval_jaxpr/ppermute | solution.py:93
  186.7 14.7 %collective-permute-done = bf16[192,30,64]{0,2,1:T(8,128)(2,1)S(1)} collective-permute-done((bf16[192,30,64]{0,2,1:T(8,128)(2,1)S(1)}, bf16[192,30,64]{0,2,1:T(8,128)(2,1)S(1)}, u32[]{:S(2)}, u32[]{:S(2)}) %collective-permute-start) | collective-permute-done | bytes 737312 | tf_op jit(solution)/shard_map/while/body/eval_jaxpr/ppermute | solution.py:93
  220.6 14.7 %collective-permute-done = bf16[192,30,64]{0,2,1:T(8,128)(2,1)S(1)} collective-permute-done((bf16[192,30,64]{0,2,1:T(8,128)(2,1)S(1)}, bf16[192,30,64]{0,2,1:T(8,128)(2,1)S(1)}, u32[]{:S(2)}, u32[]{:S(2)}) %collective-permute-start) | collective-permute-done | bytes 737312 | tf_op jit(solution)/shard_map/while/body/eval_jaxpr/ppermute | solution.py:93
  254.5 14.7 %collective-permute-done = bf16[192,30,64]{0,2,1:T(8,128)(2,1)S(1)} collective-permute-done((bf16[192,30,64]{0,2,1:T(8,128)(2,1)S(1)}, bf16[192,30,64]{0,2,1:T(8,128)(2,1)S(1)}, u32[]{:S(2)}, u32[]{:S(2)}) %collective-permute-start) | collective-permute-done | bytes 737312 | tf_op jit(solution)/shard_map/while/body/eval_jaxpr/ppermute | solution.py:93
  288.4 14.7 %collective-permute-done = bf16[192,30,64]{0,2,1:T(8,128)(2,1)S(1)} collective-permute-done((bf16[192,30,64]{0,2,1:T(8,128)(2,1)S(1)}, bf16[192,30,64]{0,2,1:T(8,128)(2,1)S(1)}, u32[]{:S(2)}, u32[]{:S(2)}) %collective-permute-start) | collective-permute-done | bytes 737312 | tf_op jit(solution)/shard_map/while/body/eval_jaxpr/ppermute | solution.py:93
  322.3 14.7 %collective-permute-done = bf16[192,30,64]{0,2,1:T(8,128)(2,1)S(1)} collective-permute-done((bf16[192,30,64]{0,2,1:T(8,128)(2,1)S(1)}, bf16[192,30,64]{0,2,1:T(8,128)(2,1)S(1)}, u32[]{:S(2)}, u32[]{:S(2)}) %collective-permute-start) | collective-permute-done | bytes 737312 | tf_op jit(solution)/shard_map/while/body/eval_jaxpr/ppermute | solution.py:93
  356.1 14.7 %collective-permute-done = bf16[192,30,64]{0,2,1:T(8,128)(2,1)S(1)} collective-permute-done((bf16[192,30,64]{0,2,1:T(8,128)(2,1)S(1)}, bf16[192,30,64]{0,2,1:T(8,128)(2,1)S(1)}, u32[]{:S(2)}, u32[]{:S(2)}) %collective-permute-start) | collective-permute-done | bytes 737312 | tf_op jit(solution)/shard_map/while/body/eval_jaxpr/ppermute | solution.py:93
  390.0 14.7 %collective-permute-done = bf16[192,30,64]{0,2,1:T(8,128)(2,1)S(1)} collective-permute-done((bf16[192,30,64]{0,2,1:T(8,128)(2,1)S(1)}, bf16[192,30,64]{0,2,1:T(8,128)(2,1)S(1)}, u32[]{:S(2)}, u32[]{:S(2)}) %collective-permute-start) | collective-permute-done | bytes 737312 | tf_op jit(solution)/shard_map/while/body/eval_jaxpr/ppermute | solution.py:93
  423.9 14.7 %collective-permute-done = bf16[192,30,64]{0,2,1:T(8,128)(2,1)S(1)} collective-permute-done((bf16[192,30,64]{0,2,1:T(8,128)(2,1)S(1)}, bf16[192,30,64]{0,2,1:T(8,128)(2,1)S(1)}, u32[]{:S(2)}, u32[]{:S(2)}) %collective-permute-start) | collective-permute-done | bytes 737312 | tf_op jit(solution)/shard_map/while/body/eval_jaxpr/ppermute | solution.py:93
  457.8 14.7 %collective-permute-done = bf16[192,30,64]{0,2,1:T(8,128)(2,1)S(1)} collective-permute-done((bf16[192,30,64]{0,2,1:T(8,128)(2,1)S(1)}, bf16[192,30,64]{0,2,1:T(8,128)(2,1)S(1)}, u32[]{:S(2)}, u32[]{:S(2)}) %collective-permute-start) | collective-permute-done | bytes 737312 | tf_op jit(solution)/shard_map/while/body/eval_jaxpr/ppermute | solution.py:93
  491.7 14.7 %collective-permute-done = bf16[192,30,64]{0,2,1:T(8,128)(2,1)S(1)} collective-permute-done((bf16[192,30,64]{0,2,1:T(8,128)(2,1)S(1)}, bf16[192,30,64]{0,2,1:T(8,128)(2,1)S(1)}, u32[]{:S(2)}, u32[]{:S(2)}) %collective-permute-start) | collective-permute-done | bytes 737312 | tf_op jit(solution)/shard_map/while/body/eval_jaxpr/ppermute | solution.py:93
  525.6 14.7 %collective-permute-done = bf16[192,30,64]{0,2,1:T(8,128)(2,1)S(1)} collective-permute-done((bf16[192,30,64]{0,2,1:T(8,128)(2,1)S(1)}, bf16[192,30,64]{0,2,1:T(8,128)(2,1)S(1)}, u32[]{:S(2)}, u32[]{:S(2)}) %collective-permute-start) | collective-permute-done | bytes 737312 | tf_op jit(solution)/shard_map/while/body/eval_jaxpr/ppermute | solution.py:93
  559.5 14.7 %collective-permute-done = bf16[192,30,64]{0,2,1:T(8,128)(2,1)S(1)} collective-permute-done((bf16[192,30,64]{0,2,1:T(8,128)(2,1)S(1)}, bf16[192,30,64]{0,2,1:T(8,128)(2,1)S(1)}, u32[]{:S(2)}, u32[]{:S(2)}) %collective-permute-start) | collective-permute-done | bytes 737312 | tf_op jit(solution)/shard_map/while/body/eval_jaxpr/ppermute | solution.py:93
  593.4 14.7 %collective-permute-done = bf16[192,30,64]{0,2,1:T(8,128)(2,1)S(1)} collective-permute-done((bf16[192,30,64]{0,2,1:T(8,128)(2,1)S(1)}, bf16[192,30,64]{0,2,1:T(8,128)(2,1)S(1)}, u32[]{:S(2)}, u32[]{:S(2)}) %collective-permute-start) | collective-permute-done | bytes 737312 | tf_op jit(solution)/shard_map/while/body/eval_jaxpr/ppermute | solution.py:93
  627.3 14.7 %collective-permute-done = bf16[192,30,64]{0,2,1:T(8,128)(2,1)S(1)} collective-permute-done((bf16[192,30,64]{0,2,1:T(8,128)(2,1)S(1)}, bf16[192,30,64]{0,2,1:T(8,128)(2,1)S(1)}, u32[]{:S(2)}, u32[]{:S(2)}) %collective-permute-start) | collective-permute-done | bytes 737312 | tf_op jit(solution)/shard_map/while/body/eval_jaxpr/ppermute | solution.py:93
  661.1 7.4 %bitcast_add_fusion = f32[418,1920]{1,0:T(8,128)S(1)} fusion(bf16[30,64,1920]{2,1,0:T(8,128)(2,1)} %bitcast.113, f32[30,418,64]{1,2,0:T(8,128)} %get-tuple-element.40, f32[30,418]{1,0:T(8,128)S(1)} %get-tuple-element.41, f32[1920]{0:T(1024)S(1)} %copy-done.31), kind=kOutput, calls=%fused_computation.39 | convolution fusion | flops 3084238080 | bytes 13851120 | tf_op jit(solution)/shard_map/hqd,hde->qe/dot_general | solution.py:99
  672.2 23.0 %fusion.18.clone.6 = bf16[418,7680]{1,0:T(8,128)(2,1)} fusion(bf16[1920,7680]{1,0:T(8,128)(2,1)} %param.36, f32[7680]{0:T(1024)S(1)} %copy-done.29, bf16[192,1920]{1,0:T(8,128)(2,1)S(1)} %fusion.78, bf16[226,1920]{1,0:T(8,128)(2,1)S(1)} %fusion.51), kind=kOutput, calls=%fused_computation.23.clone.clone.clone.clone.clone.1 | convolution fusion | flops 12362634240 | bytes 37547520 | tf_op jit(solution)/shard_map/dot_general | solution.py:68
  695.2 19.5 %fusion.29 = f32[418,1920]{1,0:T(8,128)S(1)} fusion(bf16[7680,1920]{1,0:T(8,128)(2,1)} %param.38, f32[1920]{0:T(1024)S(1)} %copy-done.32, bf16[418,7680]{1,0:T(8,128)(2,1)} %fusion.18.clone.6), kind=kOutput, calls=%fused_computation.40 | convolution fusion | flops 12328124416 | bytes 39129600 | tf_op jit(solution)/shard_map/dot_general | solution.py:70
  (383 shorter events, 380.8 us)
Async XLA Ops:
  148.9 18.6 %collective-permute-start = (bf16[192,30,64]{0,2,1:T(8,128)(2,1)S(1)}, bf16[192,30,64]{0,2,1:T(8,128)(2,1)S(1)}, u32[]{:S(2)}, u32[]{:S(2)}) collective-permute-start(bf16[192,30,64]{0,2,1:T(8,128)(2,1)S(1)} %get-tuple-element.174), channel_id=1, source_target_pairs={{0,1},{1,2},{2,3},{3,4},{4,5},{5,6},{6,7},{7,8},{8,9},{9,10},{10,1... | collective-permute-start | bytes 2211848 | tf_op jit(solution)/shard_map/while/body/eval_jaxpr/ppermute | solution.py:93
  149.0 29.1 %collective-permute-start.1 = (bf16[192,30,64]{0,2,1:T(8,128)(2,1)}, bf16[192,30,64]{0,2,1:T(8,128)(2,1)S(1)}, u32[]{:S(2)}, u32[]{:S(2)}) collective-permute-start(bf16[192,30,64]{0,2,1:T(8,128)(2,1)} %get-tuple-element.175), channel_id=1, source_target_pairs={{0,1},{1,2},{2,3},{3,4},{4,5},{5,6},{6,7},{7,8},{8,9},{9,10},{10,1... | collective-permute-start | bytes 2211848 | tf_op jit(solution)/shard_map/while/body/eval_jaxpr/ppermute | solution.py:93
  186.7 14.7 %collective-permute-start = (bf16[192,30,64]{0,2,1:T(8,128)(2,1)S(1)}, bf16[192,30,64]{0,2,1:T(8,128)(2,1)S(1)}, u32[]{:S(2)}, u32[]{:S(2)}) collective-permute-start(bf16[192,30,64]{0,2,1:T(8,128)(2,1)S(1)} %get-tuple-element.174), channel_id=1, source_target_pairs={{0,1},{1,2},{2,3},{3,4},{4,5},{5,6},{6,7},{7,8},{8,9},{9,10},{10,1... | collective-permute-start | bytes 2211848 | tf_op jit(solution)/shard_map/while/body/eval_jaxpr/ppermute | solution.py:93
  186.7 25.3 %collective-permute-start.1 = (bf16[192,30,64]{0,2,1:T(8,128)(2,1)}, bf16[192,30,64]{0,2,1:T(8,128)(2,1)S(1)}, u32[]{:S(2)}, u32[]{:S(2)}) collective-permute-start(bf16[192,30,64]{0,2,1:T(8,128)(2,1)} %get-tuple-element.175), channel_id=1, source_target_pairs={{0,1},{1,2},{2,3},{3,4},{4,5},{5,6},{6,7},{7,8},{8,9},{9,10},{10,1... | collective-permute-start | bytes 2211848 | tf_op jit(solution)/shard_map/while/body/eval_jaxpr/ppermute | solution.py:93
  220.6 14.7 %collective-permute-start = (bf16[192,30,64]{0,2,1:T(8,128)(2,1)S(1)}, bf16[192,30,64]{0,2,1:T(8,128)(2,1)S(1)}, u32[]{:S(2)}, u32[]{:S(2)}) collective-permute-start(bf16[192,30,64]{0,2,1:T(8,128)(2,1)S(1)} %get-tuple-element.174), channel_id=1, source_target_pairs={{0,1},{1,2},{2,3},{3,4},{4,5},{5,6},{6,7},{7,8},{8,9},{9,10},{10,1... | collective-permute-start | bytes 2211848 | tf_op jit(solution)/shard_map/while/body/eval_jaxpr/ppermute | solution.py:93
  220.6 25.3 %collective-permute-start.1 = (bf16[192,30,64]{0,2,1:T(8,128)(2,1)}, bf16[192,30,64]{0,2,1:T(8,128)(2,1)S(1)}, u32[]{:S(2)}, u32[]{:S(2)}) collective-permute-start(bf16[192,30,64]{0,2,1:T(8,128)(2,1)} %get-tuple-element.175), channel_id=1, source_target_pairs={{0,1},{1,2},{2,3},{3,4},{4,5},{5,6},{6,7},{7,8},{8,9},{9,10},{10,1... | collective-permute-start | bytes 2211848 | tf_op jit(solution)/shard_map/while/body/eval_jaxpr/ppermute | solution.py:93
  254.5 25.3 %collective-permute-start.1 = (bf16[192,30,64]{0,2,1:T(8,128)(2,1)}, bf16[192,30,64]{0,2,1:T(8,128)(2,1)S(1)}, u32[]{:S(2)}, u32[]{:S(2)}) collective-permute-start(bf16[192,30,64]{0,2,1:T(8,128)(2,1)} %get-tuple-element.175), channel_id=1, source_target_pairs={{0,1},{1,2},{2,3},{3,4},{4,5},{5,6},{6,7},{7,8},{8,9},{9,10},{10,1... | collective-permute-start | bytes 2211848 | tf_op jit(solution)/shard_map/while/body/eval_jaxpr/ppermute | solution.py:93
  288.4 14.7 %collective-permute-start = (bf16[192,30,64]{0,2,1:T(8,128)(2,1)S(1)}, bf16[192,30,64]{0,2,1:T(8,128)(2,1)S(1)}, u32[]{:S(2)}, u32[]{:S(2)}) collective-permute-start(bf16[192,30,64]{0,2,1:T(8,128)(2,1)S(1)} %get-tuple-element.174), channel_id=1, source_target_pairs={{0,1},{1,2},{2,3},{3,4},{4,5},{5,6},{6,7},{7,8},{8,9},{9,10},{10,1... | collective-permute-start | bytes 2211848 | tf_op jit(solution)/shard_map/while/body/eval_jaxpr/ppermute | solution.py:93
  288.4 25.3 %collective-permute-start.1 = (bf16[192,30,64]{0,2,1:T(8,128)(2,1)}, bf16[192,30,64]{0,2,1:T(8,128)(2,1)S(1)}, u32[]{:S(2)}, u32[]{:S(2)}) collective-permute-start(bf16[192,30,64]{0,2,1:T(8,128)(2,1)} %get-tuple-element.175), channel_id=1, source_target_pairs={{0,1},{1,2},{2,3},{3,4},{4,5},{5,6},{6,7},{7,8},{8,9},{9,10},{10,1... | collective-permute-start | bytes 2211848 | tf_op jit(solution)/shard_map/while/body/eval_jaxpr/ppermute | solution.py:93
  322.3 25.3 %collective-permute-start.1 = (bf16[192,30,64]{0,2,1:T(8,128)(2,1)}, bf16[192,30,64]{0,2,1:T(8,128)(2,1)S(1)}, u32[]{:S(2)}, u32[]{:S(2)}) collective-permute-start(bf16[192,30,64]{0,2,1:T(8,128)(2,1)} %get-tuple-element.175), channel_id=1, source_target_pairs={{0,1},{1,2},{2,3},{3,4},{4,5},{5,6},{6,7},{7,8},{8,9},{9,10},{10,1... | collective-permute-start | bytes 2211848 | tf_op jit(solution)/shard_map/while/body/eval_jaxpr/ppermute | solution.py:93
  356.1 25.3 %collective-permute-start.1 = (bf16[192,30,64]{0,2,1:T(8,128)(2,1)}, bf16[192,30,64]{0,2,1:T(8,128)(2,1)S(1)}, u32[]{:S(2)}, u32[]{:S(2)}) collective-permute-start(bf16[192,30,64]{0,2,1:T(8,128)(2,1)} %get-tuple-element.175), channel_id=1, source_target_pairs={{0,1},{1,2},{2,3},{3,4},{4,5},{5,6},{6,7},{7,8},{8,9},{9,10},{10,1... | collective-permute-start | bytes 2211848 | tf_op jit(solution)/shard_map/while/body/eval_jaxpr/ppermute | solution.py:93
  390.0 14.7 %collective-permute-start = (bf16[192,30,64]{0,2,1:T(8,128)(2,1)S(1)}, bf16[192,30,64]{0,2,1:T(8,128)(2,1)S(1)}, u32[]{:S(2)}, u32[]{:S(2)}) collective-permute-start(bf16[192,30,64]{0,2,1:T(8,128)(2,1)S(1)} %get-tuple-element.174), channel_id=1, source_target_pairs={{0,1},{1,2},{2,3},{3,4},{4,5},{5,6},{6,7},{7,8},{8,9},{9,10},{10,1... | collective-permute-start | bytes 2211848 | tf_op jit(solution)/shard_map/while/body/eval_jaxpr/ppermute | solution.py:93
  390.0 25.3 %collective-permute-start.1 = (bf16[192,30,64]{0,2,1:T(8,128)(2,1)}, bf16[192,30,64]{0,2,1:T(8,128)(2,1)S(1)}, u32[]{:S(2)}, u32[]{:S(2)}) collective-permute-start(bf16[192,30,64]{0,2,1:T(8,128)(2,1)} %get-tuple-element.175), channel_id=1, source_target_pairs={{0,1},{1,2},{2,3},{3,4},{4,5},{5,6},{6,7},{7,8},{8,9},{9,10},{10,1... | collective-permute-start | bytes 2211848 | tf_op jit(solution)/shard_map/while/body/eval_jaxpr/ppermute | solution.py:93
  423.9 25.3 %collective-permute-start.1 = (bf16[192,30,64]{0,2,1:T(8,128)(2,1)}, bf16[192,30,64]{0,2,1:T(8,128)(2,1)S(1)}, u32[]{:S(2)}, u32[]{:S(2)}) collective-permute-start(bf16[192,30,64]{0,2,1:T(8,128)(2,1)} %get-tuple-element.175), channel_id=1, source_target_pairs={{0,1},{1,2},{2,3},{3,4},{4,5},{5,6},{6,7},{7,8},{8,9},{9,10},{10,1... | collective-permute-start | bytes 2211848 | tf_op jit(solution)/shard_map/while/body/eval_jaxpr/ppermute | solution.py:93
  457.8 14.7 %collective-permute-start = (bf16[192,30,64]{0,2,1:T(8,128)(2,1)S(1)}, bf16[192,30,64]{0,2,1:T(8,128)(2,1)S(1)}, u32[]{:S(2)}, u32[]{:S(2)}) collective-permute-start(bf16[192,30,64]{0,2,1:T(8,128)(2,1)S(1)} %get-tuple-element.174), channel_id=1, source_target_pairs={{0,1},{1,2},{2,3},{3,4},{4,5},{5,6},{6,7},{7,8},{8,9},{9,10},{10,1... | collective-permute-start | bytes 2211848 | tf_op jit(solution)/shard_map/while/body/eval_jaxpr/ppermute | solution.py:93
  457.8 25.3 %collective-permute-start.1 = (bf16[192,30,64]{0,2,1:T(8,128)(2,1)}, bf16[192,30,64]{0,2,1:T(8,128)(2,1)S(1)}, u32[]{:S(2)}, u32[]{:S(2)}) collective-permute-start(bf16[192,30,64]{0,2,1:T(8,128)(2,1)} %get-tuple-element.175), channel_id=1, source_target_pairs={{0,1},{1,2},{2,3},{3,4},{4,5},{5,6},{6,7},{7,8},{8,9},{9,10},{10,1... | collective-permute-start | bytes 2211848 | tf_op jit(solution)/shard_map/while/body/eval_jaxpr/ppermute | solution.py:93
  491.7 25.3 %collective-permute-start.1 = (bf16[192,30,64]{0,2,1:T(8,128)(2,1)}, bf16[192,30,64]{0,2,1:T(8,128)(2,1)S(1)}, u32[]{:S(2)}, u32[]{:S(2)}) collective-permute-start(bf16[192,30,64]{0,2,1:T(8,128)(2,1)} %get-tuple-element.175), channel_id=1, source_target_pairs={{0,1},{1,2},{2,3},{3,4},{4,5},{5,6},{6,7},{7,8},{8,9},{9,10},{10,1... | collective-permute-start | bytes 2211848 | tf_op jit(solution)/shard_map/while/body/eval_jaxpr/ppermute | solution.py:93
  525.6 14.7 %collective-permute-start = (bf16[192,30,64]{0,2,1:T(8,128)(2,1)S(1)}, bf16[192,30,64]{0,2,1:T(8,128)(2,1)S(1)}, u32[]{:S(2)}, u32[]{:S(2)}) collective-permute-start(bf16[192,30,64]{0,2,1:T(8,128)(2,1)S(1)} %get-tuple-element.174), channel_id=1, source_target_pairs={{0,1},{1,2},{2,3},{3,4},{4,5},{5,6},{6,7},{7,8},{8,9},{9,10},{10,1... | collective-permute-start | bytes 2211848 | tf_op jit(solution)/shard_map/while/body/eval_jaxpr/ppermute | solution.py:93
  525.6 25.3 %collective-permute-start.1 = (bf16[192,30,64]{0,2,1:T(8,128)(2,1)}, bf16[192,30,64]{0,2,1:T(8,128)(2,1)S(1)}, u32[]{:S(2)}, u32[]{:S(2)}) collective-permute-start(bf16[192,30,64]{0,2,1:T(8,128)(2,1)} %get-tuple-element.175), channel_id=1, source_target_pairs={{0,1},{1,2},{2,3},{3,4},{4,5},{5,6},{6,7},{7,8},{8,9},{9,10},{10,1... | collective-permute-start | bytes 2211848 | tf_op jit(solution)/shard_map/while/body/eval_jaxpr/ppermute | solution.py:93
  559.5 25.3 %collective-permute-start.1 = (bf16[192,30,64]{0,2,1:T(8,128)(2,1)}, bf16[192,30,64]{0,2,1:T(8,128)(2,1)S(1)}, u32[]{:S(2)}, u32[]{:S(2)}) collective-permute-start(bf16[192,30,64]{0,2,1:T(8,128)(2,1)} %get-tuple-element.175), channel_id=1, source_target_pairs={{0,1},{1,2},{2,3},{3,4},{4,5},{5,6},{6,7},{7,8},{8,9},{9,10},{10,1... | collective-permute-start | bytes 2211848 | tf_op jit(solution)/shard_map/while/body/eval_jaxpr/ppermute | solution.py:93
  593.4 14.7 %collective-permute-start = (bf16[192,30,64]{0,2,1:T(8,128)(2,1)S(1)}, bf16[192,30,64]{0,2,1:T(8,128)(2,1)S(1)}, u32[]{:S(2)}, u32[]{:S(2)}) collective-permute-start(bf16[192,30,64]{0,2,1:T(8,128)(2,1)S(1)} %get-tuple-element.174), channel_id=1, source_target_pairs={{0,1},{1,2},{2,3},{3,4},{4,5},{5,6},{6,7},{7,8},{8,9},{9,10},{10,1... | collective-permute-start | bytes 2211848 | tf_op jit(solution)/shard_map/while/body/eval_jaxpr/ppermute | solution.py:93
  593.4 25.3 %collective-permute-start.1 = (bf16[192,30,64]{0,2,1:T(8,128)(2,1)}, bf16[192,30,64]{0,2,1:T(8,128)(2,1)S(1)}, u32[]{:S(2)}, u32[]{:S(2)}) collective-permute-start(bf16[192,30,64]{0,2,1:T(8,128)(2,1)} %get-tuple-element.175), channel_id=1, source_target_pairs={{0,1},{1,2},{2,3},{3,4},{4,5},{5,6},{6,7},{7,8},{8,9},{9,10},{10,1... | collective-permute-start | bytes 2211848 | tf_op jit(solution)/shard_map/while/body/eval_jaxpr/ppermute | solution.py:93
  627.2 14.7 %collective-permute-start = (bf16[192,30,64]{0,2,1:T(8,128)(2,1)S(1)}, bf16[192,30,64]{0,2,1:T(8,128)(2,1)S(1)}, u32[]{:S(2)}, u32[]{:S(2)}) collective-permute-start(bf16[192,30,64]{0,2,1:T(8,128)(2,1)S(1)} %get-tuple-element.174), channel_id=1, source_target_pairs={{0,1},{1,2},{2,3},{3,4},{4,5},{5,6},{6,7},{7,8},{8,9},{9,10},{10,1... | collective-permute-start | bytes 2211848 | tf_op jit(solution)/shard_map/while/body/eval_jaxpr/ppermute | solution.py:93
  627.2 25.3 %collective-permute-start.1 = (bf16[192,30,64]{0,2,1:T(8,128)(2,1)}, bf16[192,30,64]{0,2,1:T(8,128)(2,1)S(1)}, u32[]{:S(2)}, u32[]{:S(2)}) collective-permute-start(bf16[192,30,64]{0,2,1:T(8,128)(2,1)} %get-tuple-element.175), channel_id=1, source_target_pairs={{0,1},{1,2},{2,3},{3,4},{4,5},{5,6},{6,7},{7,8},{8,9},{9,10},{10,1... | collective-permute-start | bytes 2211848 | tf_op jit(solution)/shard_map/while/body/eval_jaxpr/ppermute | solution.py:93
  (84 other events, 925.7 us)
where the time goes:
time: 723 us; the launch traced here: 717 us
  waiting for transfers between devices  262 us (36%)
  matrix products  235 us (33%)
  local copies, waits for them, and re-layouts  122 us (17%)
  other arithmetic  92.9 us (13%)
    ppermute x30, waiting for transfers between devices, pass_step(): kv_blk = lax.ppermute(kv_blk, 'cp', shift_pairs)  262 us
    dot_general x16, matrix products, attend_update(): jnp.einsum('hqk,khd->hqd', attn_prob.astype(jnp.bfloat16), val_blk, prefe...  98.2 us
    while x135, local copies, waits for them, and re-layouts  76.5 us
    dot_general x16, matrix products, attend_update(): jnp.einsum('qhd,khd->hqk', queries, key_blk, preferred_element_type=jnp.f...  60.2 us
    reduce_sum x16, other arithmetic, attend_update(): new_sum = run_sum * rescale + jnp.sum(attn_prob, axis=-1)  45.2 us
    dot_general x1, matrix products, block_tail(): up_proj = jnp.dot(tokens, w_up, preferred_element_type=jnp.float32) + b_up  23 us
    split x5, local copies, waits for them, and re-layouts, project_qkv(): q_raw, k_raw, v_raw = jnp.split(qkv_all, 3, axis=-1)  20.3 us
    dot_general x1, matrix products, block_tail(): jnp.dot(gelu_out, w_down, preferred_element_type=jnp.float32) + b_down  19.5 us
  transfers between devices with their start and end apart: 30, of which 30 were waited for; matrix products, arithmetic and copies ran while one was open for 12% of the time, Pallas kernels for 0%

commit v1 on v0

v1 whole, which is shorter than its diff:
```python
import functools

import jax
import jax.numpy as jnp
from jax import lax
from jax.experimental import pallas as pl
from jax.experimental.pallas import tpu as pltpu
from jax.sharding import PartitionSpec as P

LN_EPS = 1e-5
QK_EPS = 1e-6
LANES = 128
MESH_ID = pl.DeviceIdType.MESH
F32 = jnp.float32
BF16 = jnp.bfloat16


def layer_norm(values, gain_vec, bias_vec, epsilon):
    mean_val = jnp.mean(values, axis=-1, keepdims=True)
    centred = values - mean_val
    var_val = jnp.mean(centred * centred, axis=-1, keepdims=True)
    return centred * lax.rsqrt(var_val + epsilon) * gain_vec + bias_vec


def modulation(time_emb, ada_w, ada_b):
    silu_in = jax.nn.silu(time_emb).astype(BF16)
    emb_all = jnp.dot(silu_in, ada_w, preferred_element_type=F32) + ada_b
    return jnp.split(emb_all, 6, axis=-1)


def ada_norm(states, norm_par, shift_row, scale_row):
    normed = layer_norm(states.astype(F32), norm_par[0], norm_par[1], LN_EPS)
    return (normed * (1.0 + scale_row) + shift_row).astype(BF16)


def pair_head_norm(raw, gain, bias, head_dim):
    low = lax.broadcasted_iota(jnp.int32, raw.shape, 1) < head_dim

    def head_mean(vals):
        low_sum = jnp.sum(jnp.where(low, vals, 0.0), axis=1, keepdims=True)
        high_sum = jnp.sum(jnp.where(low, 0.0, vals), axis=1, keepdims=True)
        return jnp.where(low, low_sum, high_sum) * (1.0 / head_dim)

    centred = raw - head_mean(raw)
    return centred * lax.rsqrt(head_mean(centred * centred) + QK_EPS) * gain + bias


def rotate_pairs(vals, cos_t, sin_t):
    even = lax.broadcasted_iota(jnp.int32, vals.shape, 1) % 2 == 0
    swapped = jnp.where(even, pltpu.roll(vals, LANES - 1, 1), pltpu.roll(vals, 1, 1))
    return vals * cos_t + swapped * sin_t


def qkv_kernel(head_dim, rope, tok_ref, wq_ref, wk_ref, wv_ref, bq_ref, bk_ref, bv_ref, norm_ref, cos_ref, sin_ref, out_ref):
    tok = tok_ref[...]
    n_sub = wq_ref.shape[1] // LANES
    q_all = jnp.dot(tok, wq_ref[...], preferred_element_type=F32) + bq_ref[...]
    k_all = jnp.dot(tok, wk_ref[...], preferred_element_type=F32) + bk_ref[...]
    v_all = jnp.dot(tok, wv_ref[...], preferred_element_type=F32) + bv_ref[...]
    for sub in range(n_sub):
        cols = slice(sub * LANES, (sub + 1) * LANES)
        q_n = pair_head_norm(q_all[:, cols], norm_ref[0:1], norm_ref[1:2], head_dim)
        k_n = pair_head_norm(k_all[:, cols], norm_ref[2:3], norm_ref[3:4], head_dim)
        if rope:
            q_n = rotate_pairs(q_n, cos_ref[...], sin_ref[...])
            k_n = rotate_pairs(k_n, cos_ref[...], sin_ref[...])
        out_ref[sub, :, 0:LANES] = (q_n.astype(BF16).astype(F32) * head_dim ** -0.5).astype(BF16)
        out_ref[sub, :, LANES:2 * LANES] = k_n.astype(BF16)
        out_ref[sub, :, 2 * LANES:] = v_all[:, cols].astype(BF16)


def qkv_video(tok, w_qkv, b_qkv, norm128, cos_t, sin_t, head_dim, n_groups):
    rows, width = tok.shape
    n_steps = 5
    per = n_groups // n_steps
    cols = per * LANES
    specs = [pl.BlockSpec((rows, width), lambda i: (0, 0))]
    for part in range(3):
        specs.append(pl.BlockSpec((width, cols), functools.partial(lambda part, i: (0, part * n_steps + i), part)))
    for part in range(3):
        specs.append(pl.BlockSpec((1, cols), functools.partial(lambda part, i: (0, part * n_steps + i), part)))
    specs += [pl.BlockSpec((4, LANES), lambda i: (0, 0)), pl.BlockSpec((rows, LANES), lambda i: (0, 0)), pl.BlockSpec((rows, LANES), lambda i: (0, 0))]
    return pl.pallas_call(
        functools.partial(qkv_kernel, head_dim, True),
        grid=(n_steps,),
        in_specs=specs,
        out_specs=pl.BlockSpec((per, rows, 3 * LANES), lambda i: (i, 0, 0)),
        out_shape=jax.ShapeDtypeStruct((n_groups, rows, 3 * LANES), BF16),
        compiler_params=pltpu.CompilerParams(vmem_limit_bytes=48 << 20),
        cost_estimate=pl.CostEstimate(flops=6 * rows * width * width, bytes_accessed=6 * width * width, transcendentals=0),
        name="qkv_video",
    )(tok, w_qkv, w_qkv, w_qkv, b_qkv, b_qkv, b_qkv, norm128, cos_t, sin_t)


def text_qkv_kernel(head_dim, own_ref, *refs):
    del own_ref
    qkv_kernel(head_dim, False, *refs)


def qkv_text(own, tok, w_qkv, b_qkv, norm128, head_dim, n_groups):
    rows, width = tok.shape
    specs = [pl.BlockSpec((rows, width), lambda i, own: (0, 0))]
    for part in range(3):
        specs.append(pl.BlockSpec((width, LANES), functools.partial(lambda part, i, own: (0, part * n_groups + own[0]), part)))
    for part in range(3):
        specs.append(pl.BlockSpec((1, LANES), functools.partial(lambda part, i, own: (0, part * n_groups + own[0]), part)))
    specs += [pl.BlockSpec((4, LANES), lambda i, own: (0, 0))] * 3
    return pl.pallas_call(
        functools.partial(text_qkv_kernel, head_dim),
        grid_spec=pltpu.PrefetchScalarGridSpec(
            num_scalar_prefetch=1,
            grid=(1,),
            in_specs=specs,
            out_specs=pl.BlockSpec((1, rows, 3 * LANES), lambda i, own: (0, 0, 0)),
        ),
        out_shape=jax.ShapeDtypeStruct((1, rows, 3 * LANES), BF16),
        name="qkv_text",
    )(own, tok, w_qkv, w_qkv, w_qkv, b_qkv, b_qkv, b_qkv, norm128, norm128, norm128)


def entry_barrier(me, size):
    sem = pltpu.get_barrier_semaphore()
    for step in range(1, size):
        pl.semaphore_signal(sem, inc=1, device_id={"cp": lax.rem(me + step, size)}, device_id_type=MESH_ID)
    pl.semaphore_wait(sem, size - 1)


def scatter_kernel(size, n_groups, send_ref, recv_ref, send_sem, recv_sem, own_sem):
    me = lax.axis_index("cp")
    entry_barrier(me, size)

    def copy_to(step):
        dest = lax.rem(me + step, size)
        return dest, pltpu.make_async_remote_copy(
            src_ref=send_ref.at[jnp.minimum(dest, n_groups - 1)], dst_ref=recv_ref.at[me],
            send_sem=send_sem.at[step], recv_sem=recv_sem.at[step], device_id={"cp": dest}, device_id_type=MESH_ID)

    for step in range(1, size):
        dest, copy = copy_to(step)
        pl.when(dest < n_groups)(copy.start)
    own = pltpu.make_async_copy(send_ref.at[jnp.minimum(me, n_groups - 1)], recv_ref.at[me], own_sem)
    own.start()
    for step in range(1, size):
        dest, copy = copy_to(step)
        pl.when(dest < n_groups)(copy.wait_send)
        pl.when(me < n_groups)(copy.wait_recv)
    own.wait()


def scatter_heads(send, size, n_groups):
    return pl.pallas_call(
        functools.partial(scatter_kernel, size, n_groups),
        in_specs=[pl.BlockSpec(memory_space=pl.ANY)],
        out_specs=pl.BlockSpec(memory_space=pl.ANY),
        out_shape=jax.ShapeDtypeStruct((size,) + send.shape[1:], BF16),
        scratch_shapes=[pltpu.SemaphoreType.DMA((size,)), pltpu.SemaphoreType.DMA((size,)), pltpu.SemaphoreType.DMA],
        compiler_params=pltpu.CompilerParams(collective_id=0, has_side_effects=True),
        name="scatter_heads",
    )(send)


def gather_kernel(size, n_groups, vid_ref, txt_ref, out_ref, send_sem, recv_sem, own_sem):
    me = lax.axis_index("cp")
    entry_barrier(me, size)
    rows = vid_ref.shape[1]
    txt_rows = txt_ref.shape[1]
    my_cols = pl.ds(pl.multiple_of(jnp.minimum(me, n_groups - 1) * LANES, LANES), LANES)

    def copies_to(step):
        dest = lax.rem(me + step, size)
        return [pltpu.make_async_remote_copy(
            src_ref=src.at[dest], dst_ref=out_ref.at[pl.ds(lo, n_rows), my_cols],
            send_sem=send_sem.at[idx, step], recv_sem=recv_sem.at[idx, step], device_id={"cp": dest}, device_id_type=MESH_ID)
            for idx, (src, lo, n_rows) in enumerate(((vid_ref, 0, rows), (txt_ref, rows, txt_rows)))]

    for step in range(1, size):
        for copy in copies_to(step):
            pl.when(me < n_groups)(copy.start)

    @pl.when(me < n_groups)
    def _():
        own = [pltpu.make_async_copy(src.at[me], out_ref.at[pl.ds(lo, n_rows), my_cols], own_sem.at[idx])
               for idx, (src, lo, n_rows) in enumerate(((vid_ref, 0, rows), (txt_ref, rows, txt_rows)))]
        for copy in own:
            copy.start()
        for copy in own:
            copy.wait()

    for step in range(1, size):
        src = lax.rem(me + size - step, size)
        for copy in copies_to(step):
            pl.when(me < n_groups)(copy.wait_send)
            pl.when(src < n_groups)(copy.wait_recv)


def gather_heads(o_vid, o_txt, size, n_groups):
    return pl.pallas_call(
        functools.partial(gather_kernel, size, n_groups),
        in_specs=[pl.BlockSpec(memory_space=pl.ANY)] * 2,
        out_specs=pl.BlockSpec(memory_space=pl.ANY),
        out_shape=jax.ShapeDtypeStruct((o_vid.shape[1] + o_txt.shape[1], n_groups * LANES), BF16),
        scratch_shapes=[pltpu.SemaphoreType.DMA((2, size)), pltpu.SemaphoreType.DMA((2, size)), pltpu.SemaphoreType.DMA((2,))],
        compiler_params=pltpu.CompilerParams(collective_id=1, has_side_effects=True),
        name="gather_heads",
    )(o_vid, o_txt)


NT_DIMS = (((1,), (1,)), ((), ()))


def attend_block(q_blk, key_of, val_t_of, chunks, n_text, head_dim):
    n_q = q_blk.shape[0]
    lane_low = lax.broadcasted_iota(jnp.int32, q_blk.shape, 1) < head_dim
    zero = jnp.zeros_like(q_blk)
    q_heads = [jnp.where(lane_low, q_blk, zero), jnp.where(lane_low, zero, q_blk)]
    state = [None, None]

    def scores_of(chunk, head):
        start, rows, is_text = chunk
        scores = lax.dot_general(key_of(start, rows), q_heads[head], NT_DIMS, preferred_element_type=F32)
        if is_text:
            valid = lax.broadcasted_iota(jnp.int32, scores.shape, 0) < n_text
            scores = jnp.where(valid, scores, -1e30)
        return scores

    steps = [(chunk, head) for chunk in chunks for head in range(2)]
    pending = scores_of(*steps[0])
    for idx, (chunk, head) in enumerate(steps):
        scores = pending
        if idx + 1 < len(steps):
            pending = scores_of(*steps[idx + 1])
        blk_max = jnp.max(scores, axis=0, keepdims=True)
        if state[head] is None:
            new_max = blk_max
        else:
            run_max, run_sum, run_acc = state[head]
            new_max = jnp.maximum(run_max, blk_max)
        prob = jnp.exp(scores - new_max)
        new_sum = jnp.sum(prob, axis=0, keepdims=True)
        val_t = val_t_of(chunk[0], chunk[1], head)
        new_acc = jnp.dot(val_t, prob.astype(BF16), preferred_element_type=F32)
        if state[head] is not None:
            rescale = jnp.exp(run_max - new_max)
            new_sum = run_sum * rescale + new_sum
            new_acc = run_acc * rescale + new_acc
        state[head] = (new_max, new_sum, new_acc)
    out_t = jnp.concatenate([state[head][2] / state[head][1] for head in range(2)], axis=0)
    return out_t.T.astype(BF16)


def attention_kernel(n_text, head_dim, q_ref, vid_ref, txt_ref, out_ref, val_t):
    txt_pad = txt_ref.shape[0]
    n_vid = vid_ref.shape[0]

    @pl.when(pl.program_id(0) == 0)
    def _():
        for lo in range(0, txt_pad, 256):
            val_t[:, lo:lo + 256] = txt_ref[lo:lo + 256, 2 * LANES:].T
        for lo in range(0, n_vid, 256):
            val_t[:, txt_pad + lo:txt_pad + lo + 256] = vid_ref[lo:lo + 256, 2 * LANES:].T

    def key_of(start, rows):
        if start < txt_pad:
            return txt_ref[start:start + rows, LANES:2 * LANES]
        return vid_ref[start - txt_pad:start - txt_pad + rows, LANES:2 * LANES]

    def val_t_of(start, rows, head):
        return val_t[head * head_dim:(head + 1) * head_dim, start:start + rows]

    step = 512
    chunks = [(0, txt_pad, True)] + [(txt_pad + lo, step, False) for lo in range(0, n_vid, step)]
    out_ref[...] = attend_block(q_ref[...], key_of, val_t_of, chunks, n_text, head_dim)


def attention(q_src, vid, txt, n_text, head_dim):
    n_q = q_src.shape[0]
    blk = 256
    n_vid = vid.shape[0]
    txt_pad = txt.shape[0]
    return pl.pallas_call(
        functools.partial(attention_kernel, n_text, head_dim),
        grid=(n_q // blk,),
        in_specs=[pl.BlockSpec((blk, LANES), lambda i: (i, 0)),
                  pl.BlockSpec((n_vid, 3 * LANES), lambda i: (0, 0)),
                  pl.BlockSpec((txt_pad, 3 * LANES), lambda i: (0, 0))],
        out_specs=pl.BlockSpec((blk, LANES), lambda i: (i, 0)),
        out_shape=jax.ShapeDtypeStruct((n_q, LANES), BF16),
        scratch_shapes=[pltpu.VMEM((LANES, txt_pad + n_vid), BF16)],
        compiler_params=pltpu.CompilerParams(vmem_limit_bytes=48 << 20),
        cost_estimate=pl.CostEstimate(flops=8 * n_q * (n_vid + txt_pad) * head_dim, bytes_accessed=4 << 20, transcendentals=0),
        name="attention",
    )(q_src, vid, txt)


def solution(mesh):
    cp_size = mesh.shape['cp']

    def device_block(video_states, text_states, time_emb, rope_angle, ada1_w, ada1_b, norm1_par, w_qkv, b_qkv, qk_norm, w_out, b_out, ada2_w, ada2_b, norm2_par, w_up, b_up, w_down, b_down):
        vid_in = video_states[0]
        txt_in = text_states[0]
        n_text = txt_in.shape[0]
        n_vid, width = vid_in.shape
        head_dim = qk_norm.shape[-1]
        n_groups = width // LANES
        me = lax.axis_index('cp')
        txt_share = -(-n_text // (16 * cp_size)) * 16
        txt_pad = jnp.pad(txt_in, ((0, txt_share * cp_size - n_text), (0, 0)))

        vid_shift, vid_scale, vid_gate, txt_shift, txt_scale, txt_gate = modulation(time_emb, ada1_w, ada1_b)
        tok_vid = ada_norm(vid_in, norm1_par, vid_shift, vid_scale)
        tok_txt = ada_norm(txt_pad, norm1_par, txt_shift, txt_scale)
        norm128 = jnp.concatenate([qk_norm, qk_norm], axis=1)
        cos_t = jnp.tile(jnp.repeat(jnp.cos(rope_angle), 2, axis=1), (1, 2))
        sin_h = jnp.sin(rope_angle)
        sin_t = jnp.tile(jnp.stack([-sin_h, sin_h], axis=-1).reshape(n_vid, head_dim), (1, 2))
        b_row = b_qkv[None]

        own = jnp.minimum(me, n_groups - 1).astype(jnp.int32)[None]
        txt_qkv = qkv_text(own, tok_txt, w_qkv, b_row, norm128, head_dim, n_groups)[0]
        send = qkv_video(tok_vid, w_qkv, b_row, norm128, cos_t, sin_t, head_dim, n_groups)
        recv = scatter_heads(send, cp_size, n_groups).reshape(cp_size * n_vid, 3 * LANES)
        o_vid = attention(recv, recv, txt_qkv, n_text, head_dim).reshape(cp_size, n_vid, LANES)
        o_txt = attention(txt_qkv, recv, txt_qkv, n_text, head_dim).reshape(cp_size, txt_share, LANES)
        att = gather_heads(o_vid, o_txt, cp_size, n_groups)

        proj = jnp.dot(att, w_out, preferred_element_type=F32) + b_out
        txt_loc = lax.dynamic_slice_in_dim(txt_pad, me * txt_share, txt_share, 0)
        is_vid = lax.broadcasted_iota(jnp.int32, (n_vid + txt_share, 1), 0) < n_vid

        def by_row(vid_row, txt_row):
            return jnp.where(is_vid, vid_row, txt_row)

        x_in = jnp.concatenate([vid_in, txt_loc], axis=0).astype(F32)
        mid = (x_in + by_row(vid_gate, txt_gate) * proj).astype(BF16)
        vid_shift, vid_scale, vid_gate2, txt_shift, txt_scale, txt_gate2 = modulation(time_emb, ada2_w, ada2_b)
        tokens = ada_norm(mid, norm2_par, by_row(vid_shift, txt_shift), by_row(vid_scale, txt_scale))
        up_proj = jnp.dot(tokens, w_up, preferred_element_type=F32) + b_up
        gelu_out = jax.nn.gelu(up_proj, approximate=True).astype(BF16)
        ffn_out = jnp.dot(gelu_out, w_down, preferred_element_type=F32) + b_down
        out = (mid.astype(F32) + by_row(vid_gate2, txt_gate2) * ffn_out).astype(BF16)
        txt_out = lax.all_gather(out[n_vid:], 'cp', axis=0, tiled=True)[:n_text]
        return out[None, :n_vid], txt_out[None]

    in_specs = (P('cfg', 'cp', None), P('cfg', None, None), P('cfg', None), P('cp', None)) + (P(),) * 15
    out_specs = (P('cfg', 'cp', None), P('cfg', None, None))
    return jax.shard_map(device_block, mesh=mesh, in_specs=in_specs, out_specs=out_specs, check_vma=False)
```

time: 723 us -> 220 us (0.30)
  the two profiles are of different devices: /device:TPU:30 before, /device:TPU:21 now
where the time goes in v1:
time: 220 us
  Pallas kernels  149 us (68%)
  matrix products  41.2 us (19%)
  blocking collectives  18.8 us (9%)
  local copies, waits for them, and re-layouts  5.82 us (3%)
  other arithmetic  3.83 us (2%)
    pallas_call x1, Pallas kernels, scatter_heads(): pl.pallas_call(functools.partial(scatter_kernel, size, n_groups), in_spec...  63.4 us
    pallas_call x2, Pallas kernels, attention(): pl.pallas_call(functools.partial(attention_kernel, n_text, head_dim), gri...  43.4 us
    pallas_call x1, Pallas kernels, gather_heads(): pl.pallas_call(functools.partial(gather_kernel, size, n_groups), in_specs...  27.2 us
    dot_general x1, matrix products, device_block(): ffn_out = jnp.dot(gelu_out, w_down, preferred_element_type=F32) + b_down  23.6 us
    all_gather x1, blocking collectives, device_block(): txt_out = lax.all_gather(out[n_vid:], 'cp', axis=0, tiled=True)[:n_text]  18.8 us
    dot_general x2, matrix products, modulation(): emb_all = jnp.dot(silu_in, ada_w, preferred_element_type=F32) + ada_b  12.1 us
    pallas_call x1, Pallas kernels, qkv_video(): pl.pallas_call(functools.partial(qkv_kernel, head_dim, True), grid=(n_ste...  11.7 us
    dot_general x1, matrix products, device_block(): proj = jnp.dot(att, w_out, preferred_element_type=F32) + b_out  5.5 us

profile of v1, /device:TPU:21, one launch (start us, length us, event | category | flops | bytes accessed | tf_op | source)
XLA Modules:
  0.0 219.9 jit_solution(3404838965936950630)
XLA Ops:
  0.7 6.1 %convolution_reduce_fusion.1 = f32[11520]{0:T(1024)S(1)} fusion(bf16[512,11520]{1,0:T(8,128)(2,1)} %param.23, f32[1,512]{1,0:T(1,128)} %param.21), kind=kOutput, calls=%fused_computation.48 | convolution fusion | flops 11799040 | bytes 11844608 | tf_op jit(solution)/shard_map/dot_general | solution.py:27
  7.0 0.2 convert_reduce_fusion.1
  7.2 0.3 fusion.32
  7.6 0.5 fusion.37.tok_ref
  8.8 11.7 %qkv_video.1.send_ref = bf16[15,192,384]{2,1,0:T(8,128)(2,1)S(1)} custom-call(bf16[192,1920]{1,0:T(8,128)(2,1)S(1)} %fusion.37.tok_ref, bf16[1920,5760]{1,0:T(8,128)(2,1)} %refs_3_.1, bf16[1920,5760]{1,0:T(8,128)(2,1)} %refs_3_.1, bf16[1920,5760]{1,0:T(8,128)(2,1)} %refs_3_.1, f32[1,5760]{1,0:T(1,128)S(1)} %broadcast_in_dim.116.bq_ref.bk_ref.bv_ref.refs_4_.refs_5_.refs_6_, ...), custom_call_target="tpu_custom_call" | custom-call | flops 4246732800 | bytes 22118400 | tf_op jit(solution)/shard_map/qkv_video/pallas_call | solution.py:83
  20.6 1.3 copy-done.1
  21.9 63.4 %scatter_heads.1 = bf16[16,192,384]{2,1,0:T(8,128)(2,1)} custom-call(bf16[15,192,384]{2,1,0:T(8,128)(2,1)} %copy-done.1), custom_call_target="tpu_custom_call" | custom-call | tf_op jit(solution)/shard_map/scatter_heads/pallas_call | solution.py:151
  85.3 0.2 convert_reduce_fusion
  85.5 0.4 fusion.24
  85.9 1.6 fusion.29.refs_0_
  87.5 3.4 %qkv_text.1 = bf16[1,256,384]{2,1,0:T(8,128)(2,1)} custom-call(s32[1]{0:T(128)} %bitcast.7.own_ref, bf16[256,1920]{1,0:T(8,128)(2,1)} %fusion.29.refs_0_, bf16[1920,5760]{1,0:T(8,128)(2,1)} %refs_3_.1, bf16[1920,5760]{1,0:T(8,128)(2,1)} %refs_3_.1, bf16[1920,5760]{1,0:T(8,128)(2,1)} %refs_3_.1, f32[1,5760]{1,0:T(1,128)} %copy-done.3, f32[1,5760]{1,0:T(1,128)} %copy-done.3, ...), custom_call_target="tpu_custom_call" | custom-call | tf_op jit(solution)/shard_map/qkv_text/pallas_call | solution.py:108
  91.0 0.9 copy-done.2
  91.9 40.1 %attention.2 = bf16[3072,128]{1,0:T(8,128)(2,1)S(1)} custom-call(bf16[3072,384]{1,0:T(8,128)(2,1)S(1)} %bitcast.34, bf16[3072,384]{1,0:T(8,128)(2,1)S(1)} %bitcast.35, bf16[256,384]{1,0:T(8,128)(2,1)S(1)} %bitcast.37), custom_call_target="tpu_custom_call" | custom-call | flops 5234491392 | bytes 4194304 | tf_op jit(solution)/shard_map/attention/pallas_call | solution.py:280
  132.0 3.3 %attention.3 = bf16[256,128]{1,0:T(8,128)(2,1)S(1)} custom-call(bf16[256,384]{1,0:T(8,128)(2,1)S(1)} %bitcast.38, bf16[3072,384]{1,0:T(8,128)(2,1)S(1)} %bitcast.36, bf16[256,384]{1,0:T(8,128)(2,1)S(1)} %bitcast.39), custom_call_target="tpu_custom_call" | custom-call | flops 436207616 | bytes 4194304 | tf_op jit(solution)/shard_map/attention/pallas_call | solution.py:280
  135.4 0.6 copy-done.5
  136.0 27.2 %gather_heads.1 = bf16[208,1920]{1,0:T(8,128)(2,1)} custom-call(bf16[16,192,128]{2,1,0:T(8,128)(2,1)} %bitcast.40, bf16[16,16,128]{2,1,0:T(8,128)(2,1)} %bitcast.41), custom_call_target="tpu_custom_call" | custom-call | tf_op jit(solution)/shard_map/gather_heads/pallas_call | solution.py:197
  163.3 5.5 %fusion.70 = (f32[208]{0:T(256)S(1)}, f32[208,1920]{1,0:T(8,128)S(1)}) fusion(f32[1920]{0:T(1024)S(1)} %copy-done.19, bf16[208,1920]{1,0:T(8,128)(2,1)} %gather_heads.1, bf16[1920,1920]{1,0:T(8,128)(2,1)} %param.29, f32[1920]{0:T(1024)S(1)} %get-tuple-element.13, f32[1920]{0:T(1024)S(1)} %get-tuple-element.8, pred[208]{0:T(512)(128)(4,1)S(1)} %iota_compare_fusion, ...), kind=kOutput, calls=%fused_computation.100 | convolution fusion | flops 1537935104 | bytes 10591760 | tf_op jit(solution)/shard_map/dot_general | solution.py:326
  168.8 6.0 %convolution_reduce_fusion = f32[11520]{0:T(1024)S(1)} fusion(bf16[512,11520]{1,0:T(8,128)(2,1)} %param.31, f32[1,512]{1,0:T(1,128)S(1)} %copy-done.14), kind=kOutput, calls=%fused_computation.47 | convolution fusion | flops 11799040 | bytes 11844608 | tf_op jit(solution)/shard_map/dot_general | solution.py:27
  175.1 0.3 multiply_reduce_fusion
  175.4 0.2 copy-done.18
  175.6 23.6 %fusion.21 = bf16[208,1920]{1,0:T(8,128)(2,1)S(1)} fusion(f32[208,1920]{1,0:T(8,128)S(1)} %get-tuple-element.21, bf16[7680,1920]{1,0:T(8,128)(2,1)} %param.36, bf16[1920,7680]{1,0:T(8,128)(2,1)} %param.34, f32[7680]{0:T(1024)S(1)} %copy-done.18, f32[1920]{0:T(1024)S(1)} %copy-done.20, f32[1920]{0:T(1024)S(1)} %get-tuple-element.3, ...), kind=kOutput, calls=%fused_computation.24 | convolution fusion | flops 12290304000 | bytes 61480272 | tf_op jit(solution)/shard_map/dot_general | solution.py:339
  199.2 0.9 slice_bitcast_fusion.1
  200.1 18.8 %all_gather.3 = bf16[256,1920]{1,0:T(8,128)(2,1)S(1)} all-gather(bf16[16,1920]{1,0:T(8,128)(2,1)S(1)} %slice.31), channel_id=1, replica_groups=mesh['cfg'=4,'cp'=16] {'cp'}, dimensions={0}, use_global_device_ids=true | all-gather | bytes 1044480 | tf_op jit(solution)/shard_map/all_gather | solution.py:341
  218.9 1.0 slice_bitcast_fusion
  (66 shorter events, 1.2 us)
Async XLA Ops:
  0.6 6.1 %copy-start.10 = (f32[11520]{0:T(1024)S(1)}, f32[11520]{0:T(1024)}, u32[]{:S(2)}) copy-start(f32[11520]{0:T(1024)} %param.24) | copy-start | bytes 138244
  0.6 6.2 %copy-start.15 = (f32[2,1920]{1,0:T(2,128)S(1)}, f32[2,1920]{1,0:T(2,128)}, u32[]{:S(2)}) copy-start(f32[2,1920]{1,0:T(2,128)} %param.25) | copy-start | bytes 46084
  0.7 6.4 %copy-start.8 = (bf16[1,192,1920]{2,1,0:T(8,128)(2,1)S(1)}, bf16[1,192,1920]{2,1,0:T(8,128)(2,1)}, u32[]{:S(2)}) copy-start(bf16[1,192,1920]{2,1,0:T(8,128)(2,1)} %param.19) | copy-start | bytes 2211844
  6.8 1.3 copy-start.13
  6.8 1.3 copy-start.17
  6.9 1.4 copy-start.12
  8.2 12.4 %copy-start.3 = (f32[1,5760]{1,0:T(1,128)}, f32[1,5760]{1,0:T(1,128)S(1)}, u32[]{:S(2)}) copy-start(f32[1,5760]{1,0:T(1,128)S(1)} %broadcast_in_dim.116.bq_ref.bk_ref.bv_ref.refs_4_.refs_5_.refs_6_) | copy-start | bytes 69124
  8.2 12.3 %copy-start.6 = (f32[4,128]{1,0:T(4,128)}, f32[4,128]{1,0:T(4,128)S(1)}, u32[]{:S(2)}) copy-start(f32[4,128]{1,0:T(4,128)S(1)} %pad_maximum_fusion.1.norm_ref.refs_7_.refs_8_.refs_9_) | copy-start | bytes 6148
  20.6 1.3 copy-start.1
  21.9 63.4 %copy-start.7 = (bf16[1,226,1920]{2,1,0:T(8,128)(2,1)S(1)}, bf16[1,226,1920]{2,1,0:T(8,128)(2,1)}, u32[]{:S(2)}) copy-start(bf16[1,226,1920]{2,1,0:T(8,128)(2,1)} %param.20) | copy-start | bytes 2603524
  87.5 3.4 %copy-start = (bf16[16,192,384]{2,1,0:T(8,128)(2,1)S(1)}, bf16[16,192,384]{2,1,0:T(8,128)(2,1)}, u32[]{:S(2)}) copy-start(bf16[16,192,384]{2,1,0:T(8,128)(2,1)} %scatter_heads.1) | copy-start | bytes 7077892
  91.0 0.9 copy-start.2
  132.0 3.3 %copy-start.4 = (bf16[3072,128]{1,0:T(8,128)(2,1)}, bf16[3072,128]{1,0:T(8,128)(2,1)S(1)}, u32[]{:S(2)}) copy-start(bf16[3072,128]{1,0:T(8,128)(2,1)S(1)} %attention.2) | copy-start | bytes 2359300
  135.4 0.6 copy-start.5
  136.0 27.3 %copy-start.9 = (bf16[1,192,1920]{2,1,0:T(8,128)(2,1)S(1)}, bf16[1,192,1920]{2,1,0:T(8,128)(2,1)}, u32[]{:S(2)}) copy-start(bf16[1,192,1920]{2,1,0:T(8,128)(2,1)} %param.19) | copy-start | bytes 2211844
  136.0 27.3 %copy-start.19 = (f32[1920]{0:T(1024)S(1)}, f32[1920]{0:T(1024)}, u32[]{:S(2)}) copy-start(f32[1920]{0:T(1024)} %param.30) | copy-start | bytes 23044
  163.3 5.5 %copy-start.14 = (f32[1,512]{1,0:T(1,128)S(1)}, f32[1,512]{1,0:T(1,128)}, u32[]{:S(2)}) copy-start(f32[1,512]{1,0:T(1,128)} %param.21) | copy-start | bytes 6148
  168.8 6.0 %copy-start.11 = (f32[11520]{0:T(1024)S(1)}, f32[11520]{0:T(1024)}, u32[]{:S(2)}) copy-start(f32[11520]{0:T(1024)} %param.32) | copy-start | bytes 138244
  168.8 6.1 %copy-start.16 = (f32[2,1920]{1,0:T(2,128)S(1)}, f32[2,1920]{1,0:T(2,128)}, u32[]{:S(2)}) copy-start(f32[2,1920]{1,0:T(2,128)} %param.33) | copy-start | bytes 46084
  174.9 0.8 copy-start.18
  174.9 0.8 copy-start.20

commit v2 on v0

v2 whole, which is shorter than its diff:
```python
import functools

import jax
import jax.numpy as jnp
from jax import lax
from jax.experimental import pallas as pl
from jax.experimental.pallas import tpu as pltpu
from jax.sharding import PartitionSpec as P

LN_EPS = 1e-5
QK_EPS = 1e-6
LANES = 128
MESH_ID = pl.DeviceIdType.MESH
F32 = jnp.float32
BF16 = jnp.bfloat16


def layer_norm(values, gain_vec, bias_vec, epsilon):
    mean_val = jnp.mean(values, axis=-1, keepdims=True)
    centred = values - mean_val
    var_val = jnp.mean(centred * centred, axis=-1, keepdims=True)
    return centred * lax.rsqrt(var_val + epsilon) * gain_vec + bias_vec


def modulation(time_emb, ada_w, ada_b):
    silu_in = jax.nn.silu(time_emb).astype(BF16)
    emb_all = jnp.dot(silu_in, ada_w, preferred_element_type=F32) + ada_b
    return jnp.split(emb_all, 6, axis=-1)


def ada_norm(states, norm_par, shift_row, scale_row):
    normed = layer_norm(states.astype(F32), norm_par[0], norm_par[1], LN_EPS)
    return (normed * (1.0 + scale_row) + shift_row).astype(BF16)


def pair_head_norm(raw, gain, bias, head_dim):
    low = lax.broadcasted_iota(jnp.int32, raw.shape, 1) < head_dim

    def head_mean(vals):
        low_sum = jnp.sum(jnp.where(low, vals, 0.0), axis=1, keepdims=True)
        high_sum = jnp.sum(jnp.where(low, 0.0, vals), axis=1, keepdims=True)
        return jnp.where(low, low_sum, high_sum) * (1.0 / head_dim)

    centred = raw - head_mean(raw)
    return centred * lax.rsqrt(head_mean(centred * centred) + QK_EPS) * gain + bias


def rotate_pairs(vals, cos_t, sin_t):
    even = lax.broadcasted_iota(jnp.int32, vals.shape, 1) % 2 == 0
    swapped = jnp.where(even, pltpu.roll(vals, LANES - 1, 1), pltpu.roll(vals, 1, 1))
    return vals * cos_t + swapped * sin_t


def entry_barrier(me, size):
    sem = pltpu.get_barrier_semaphore()
    for step in range(1, size):
        pl.semaphore_signal(sem, inc=1, device_id={"cp": lax.rem(me + step, size)}, device_id_type=MESH_ID)
    pl.semaphore_wait(sem, size - 1)


NT_DIMS = (((1,), (1,)), ((), ()))


def attend_block(q_blk, key_of, val_t_of, chunks, n_text, head_dim):
    lane_low = lax.broadcasted_iota(jnp.int32, q_blk.shape, 1) < head_dim
    zero = jnp.zeros_like(q_blk)
    q_heads = [jnp.where(lane_low, q_blk, zero), jnp.where(lane_low, zero, q_blk)]
    state = [None, None]

    def scores_of(chunk, head):
        start, rows, is_text = chunk
        scores = lax.dot_general(key_of(start, rows), q_heads[head], NT_DIMS, preferred_element_type=F32)
        if is_text:
            valid = lax.broadcasted_iota(jnp.int32, scores.shape, 0) < n_text
            scores = jnp.where(valid, scores, -1e30)
        return scores

    steps = [(chunk, head) for chunk in chunks for head in range(2)]
    pending = scores_of(*steps[0])
    for idx, (chunk, head) in enumerate(steps):
        scores = pending
        if idx + 1 < len(steps):
            pending = scores_of(*steps[idx + 1])
        blk_max = jnp.max(scores, axis=0, keepdims=True)
        if state[head] is None:
            new_max = blk_max
        else:
            run_max, run_sum, run_acc = state[head]
            new_max = jnp.maximum(run_max, blk_max)
        prob = jnp.exp(scores - new_max)
        new_sum = jnp.sum(prob, axis=0, keepdims=True)
        val_t = val_t_of(chunk[0], chunk[1], head)
        new_acc = jnp.dot(val_t, prob.astype(BF16), preferred_element_type=F32)
        if state[head] is not None:
            rescale = jnp.exp(run_max - new_max)
            new_sum = run_sum * rescale + new_sum
            new_acc = run_acc * rescale + new_acc
        state[head] = (new_max, new_sum, new_acc)
    out_t = jnp.concatenate([state[head][2] / state[head][1] for head in range(2)], axis=0)
    return out_t.T.astype(BF16)


TILE_GROUPS = 3
W_SLOTS = 4
Q_BLK = 256
SRC_PER_Q = 4


def attention_kernel(size, n_groups, n_text, head_dim, tok_ref, txt_ref, w_ref, b_ref, norm_ref, cos_ref, sin_ref, out_ref,
                     w_buf, wt_buf, kv_send, q_send, kv_all, q_all, o_all, val_t, att,
                     w_sem, wt_sem, kv_ssem, kv_rsem, q_ssem, q_rsem, ov_ssem, ov_rsem, ot_ssem, ot_rsem):
    me = lax.axis_index("cp")
    owner = me < n_groups
    rows, width = tok_ref.shape
    txt_pad = txt_ref.shape[0]
    txt_share = txt_pad // size
    tile_cols = TILE_GROUPS * LANES
    n_tiles = n_groups // TILE_GROUPS
    scale = head_dim ** -0.5

    def tile_col(t):
        is_q = (t >= 2 * n_tiles)
        if isinstance(t, int):
            return (t - 2 * n_tiles) * tile_cols if is_q else width * (1 + t % 2) + (t // 2) * tile_cols
        return jnp.where(is_q, (t - 2 * n_tiles) * tile_cols, width * (1 + lax.rem(t, 2)) + (t // 2) * tile_cols)

    def w_copy(t):
        col = tile_col(t)
        slot = lax.rem(t, W_SLOTS)
        return pltpu.make_async_copy(w_ref.at[:, pl.ds(pl.multiple_of(col, LANES), tile_cols)], w_buf.at[slot], w_sem.at[slot])

    mine = jnp.minimum(me, n_groups - 1)

    def wt_copy(part):
        return pltpu.make_async_copy(w_ref.at[:, pl.ds(pl.multiple_of(part * width + mine * LANES, LANES), LANES)], wt_buf.at[part], wt_sem.at[part])

    for t in range(W_SLOTS - 1):
        w_copy(jnp.int32(t)).start()
    for part in range(3):
        wt_copy(part).start()
    entry_barrier(me, size)

    def norm_q(raw):
        return pair_head_norm(raw, norm_ref[0:1], norm_ref[1:2], head_dim)

    def norm_k(raw):
        return pair_head_norm(raw, norm_ref[2:3], norm_ref[3:4], head_dim)

    def scaled(q_n):
        return (q_n.astype(BF16).astype(F32) * scale).astype(BF16)

    def bias_at(col, n_cols):
        return b_ref[:, pl.ds(pl.multiple_of(col, LANES), n_cols)]

    def kv_copy(grp):
        return pltpu.make_async_remote_copy(
            src_ref=kv_send.at[grp], dst_ref=kv_all.at[pl.ds(pl.multiple_of(txt_pad + rows * me, 16), rows)],
            send_sem=kv_ssem.at[grp], recv_sem=kv_rsem.at[me], device_id={"cp": grp}, device_id_type=MESH_ID)

    def kv_arrival(src):
        return pltpu.make_async_remote_copy(
            src_ref=kv_send.at[0], dst_ref=kv_all.at[pl.ds(txt_pad + rows * src, rows)],
            send_sem=kv_ssem.at[0], recv_sem=kv_rsem.at[src], device_id={"cp": mine}, device_id_type=MESH_ID)

    def q_copy(grp):
        return pltpu.make_async_remote_copy(
            src_ref=q_send.at[grp], dst_ref=q_all.at[pl.ds(pl.multiple_of(txt_pad + rows * me, 16), rows)],
            send_sem=q_ssem.at[grp], recv_sem=q_rsem.at[me], device_id={"cp": grp}, device_id_type=MESH_ID)

    def q_arrival(src):
        return pltpu.make_async_remote_copy(
            src_ref=q_send.at[0], dst_ref=q_all.at[pl.ds(pl.multiple_of(txt_pad + rows * src, 16), rows)],
            send_sem=q_ssem.at[0], recv_sem=q_rsem.at[src], device_id={"cp": mine}, device_id_type=MESH_ID)

    def kv_tile(i, _):
        t_k = 2 * i
        t_v = 2 * i + 1
        w_copy(t_k).wait()
        w_copy(t_k + 3).start()
        k_all = jnp.dot(tok_ref[...], w_buf[lax.rem(t_k, W_SLOTS)], preferred_element_type=F32) + bias_at(width + i * tile_cols, tile_cols)
        for sub in range(TILE_GROUPS):
            k_n = rotate_pairs(norm_k(k_all[:, sub * LANES:(sub + 1) * LANES]), cos_ref[...], sin_ref[...])
            kv_send[i * TILE_GROUPS + sub, :, 0:LANES] = k_n.astype(BF16)
        w_copy(t_v).wait()
        w_copy(t_v + 3).start()
        v_all = jnp.dot(tok_ref[...], w_buf[lax.rem(t_v, W_SLOTS)], preferred_element_type=F32) + bias_at(2 * width + i * tile_cols, tile_cols)
        for sub in range(TILE_GROUPS):
            kv_send[i * TILE_GROUPS + sub, :, LANES:] = v_all[:, sub * LANES:(sub + 1) * LANES].astype(BF16)
        for sub in range(TILE_GROUPS):
            grp = i * TILE_GROUPS + sub
            pl.when(grp != me)(kv_copy(grp).start)
        return 0

    lax.fori_loop(0, n_tiles, kv_tile, 0)

    def q_tile(i, _):
        t_q = 2 * n_tiles + i
        w_copy(t_q).wait()

        @pl.when(t_q + 3 < 3 * n_tiles)
        def _():
            w_copy(t_q + 3).start()

        q_proj = jnp.dot(tok_ref[...], w_buf[lax.rem(t_q, W_SLOTS)], preferred_element_type=F32) + bias_at(i * tile_cols, tile_cols)
        for sub in range(TILE_GROUPS):
            q_n = rotate_pairs(norm_q(q_proj[:, sub * LANES:(sub + 1) * LANES]), cos_ref[...], sin_ref[...])
            q_send[i * TILE_GROUPS + sub] = scaled(q_n)
        for sub in range(TILE_GROUPS):
            grp = i * TILE_GROUPS + sub
            pl.when(grp != me)(q_copy(grp).start)
        return 0

    lax.fori_loop(0, n_tiles, q_tile, 0)

    for part in range(3):
        wt_copy(part).wait()
    t_proj = [jnp.dot(txt_ref[...], wt_buf[part], preferred_element_type=F32) + bias_at(part * width + mine * LANES, LANES) for part in range(3)]
    q_all[0:txt_pad] = scaled(norm_q(t_proj[0]))
    kv_all[0:txt_pad, 0:LANES] = norm_k(t_proj[1]).astype(BF16)
    kv_all[0:txt_pad, LANES:] = t_proj[2].astype(BF16)

    def ov_copy(dest):
        return pltpu.make_async_remote_copy(
            src_ref=o_all.at[pl.ds(pl.multiple_of(txt_pad + rows * dest, 16), rows)], dst_ref=att.at[mine, pl.ds(0, rows)],
            send_sem=ov_ssem.at[dest], recv_sem=ov_rsem.at[mine], device_id={"cp": dest}, device_id_type=MESH_ID)

    def ot_copy(dest):
        return pltpu.make_async_remote_copy(
            src_ref=o_all.at[pl.ds(pl.multiple_of(txt_share * dest, 16), txt_share)], dst_ref=att.at[mine, pl.ds(rows, txt_share)],
            send_sem=ot_ssem.at[dest], recv_sem=ot_rsem.at[mine], device_id={"cp": dest}, device_id_type=MESH_ID)

    def o_arrival(src):
        return [pltpu.make_async_remote_copy(
            src_ref=o_all.at[pl.ds(0, n_rows)], dst_ref=att.at[src, pl.ds(lo, n_rows)],
            send_sem=ssem.at[0], recv_sem=rsem.at[src], device_id={"cp": mine}, device_id_type=MESH_ID)
            for ssem, rsem, lo, n_rows in ((ov_ssem, ov_rsem, 0, rows), (ot_ssem, ot_rsem, rows, txt_share))]

    n_all = txt_pad + rows * size

    @pl.when(owner)
    def _():
        own_rows = pl.ds(pl.multiple_of(txt_pad + rows * mine, 16), rows)
        kv_all[own_rows] = kv_send[mine]
        q_all[own_rows] = q_send[mine]
        val_t[:, 0:txt_pad] = kv_all[0:txt_pad, LANES:].T
        for chip in range(size // 2):
            for src in (2 * chip, 2 * chip + 1):
                pl.when(src != me)(kv_arrival(src).wait_recv)
            lo = txt_pad + 2 * rows * chip
            val_t[:, lo:lo + 2 * rows] = kv_all[lo:lo + 2 * rows, LANES:].T

        step = 512
        chunks = [(0, txt_pad, True)] + [(lo, step, False) for lo in range(txt_pad, n_all, step)]
        per_group = SRC_PER_Q * rows // Q_BLK

        def block(blk, _):
            vid_idx = blk - 1
            group = vid_idx // per_group

            @pl.when((blk > 0) & (lax.rem(vid_idx + per_group, per_group) == 0))
            def _():
                for idx in range(SRC_PER_Q):
                    src = group * SRC_PER_Q + idx
                    pl.when(src != me)(q_arrival(src).wait_recv)

            lo = pl.multiple_of(blk * Q_BLK, Q_BLK)
            o_all[pl.ds(lo, Q_BLK)] = attend_block(
                q_all[pl.ds(lo, Q_BLK)],
                lambda start, n_rows: kv_all[start:start + n_rows, 0:LANES],
                lambda start, n_rows, head: val_t[head * head_dim:(head + 1) * head_dim, start:start + n_rows],
                chunks, n_text, head_dim)

            @pl.when(blk == 0)
            def _():
                for dest in range(size):
                    pl.when(dest != me)(ot_copy(dest).start)

            @pl.when((blk > 0) & (lax.rem(vid_idx + per_group, per_group) == per_group - 1))
            def _():
                for idx in range(SRC_PER_Q):
                    dest = group * SRC_PER_Q + idx
                    pl.when(dest != me)(ov_copy(dest).start)

            return 0

        lax.fori_loop(0, n_all // Q_BLK, block, 0)
        att[mine, 0:rows] = o_all[own_rows]
        att[mine, rows:] = o_all[pl.ds(pl.multiple_of(txt_share * mine, 16), txt_share)]

    for src in range(n_groups):
        @pl.when(src != me)
        def _():
            for copy in o_arrival(src):
                copy.wait_recv()

        out_ref[:, src * LANES:(src + 1) * LANES] = att[src]

    for grp in range(n_groups):
        @pl.when(grp != me)
        def _():
            kv_copy(grp).wait_send()
            q_copy(grp).wait_send()

    for dest in range(size):
        @pl.when(owner & (dest != me))
        def _():
            ov_copy(dest).wait_send()
            ot_copy(dest).wait_send()


def attention(tok, txt, w_qkv, b_qkv, norm128, cos_t, sin_t, size, n_text, head_dim):
    rows, width = tok.shape
    txt_pad = txt.shape[0]
    n_groups = width // LANES
    n_all = txt_pad + rows * size
    out_rows = rows + txt_pad // size
    vmem = pl.BlockSpec(memory_space=pltpu.VMEM)
    dma = pltpu.SemaphoreType.DMA
    return pl.pallas_call(
        functools.partial(attention_kernel, size, n_groups, n_text, head_dim),
        in_specs=[vmem, vmem, pl.BlockSpec(memory_space=pl.ANY), vmem, vmem, vmem, vmem],
        out_specs=vmem,
        out_shape=jax.ShapeDtypeStruct((out_rows, width), BF16),
        scratch_shapes=[
            pltpu.VMEM((W_SLOTS, width, TILE_GROUPS * LANES), BF16),
            pltpu.VMEM((3, width, LANES), BF16),
            pltpu.VMEM((n_groups, rows, 2 * LANES), BF16),
            pltpu.VMEM((n_groups, rows, LANES), BF16),
            pltpu.VMEM((n_all, 2 * LANES), BF16),
            pltpu.VMEM((n_all, LANES), BF16),
            pltpu.VMEM((n_all, LANES), BF16),
            pltpu.VMEM((LANES, n_all), BF16),
            pltpu.VMEM((n_groups, out_rows, LANES), BF16),
            dma((W_SLOTS,)), dma((3,)),
            dma((n_groups,)), dma((size,)), dma((n_groups,)), dma((size,)),
            dma((size,)), dma((n_groups,)), dma((size,)), dma((n_groups,)),
        ],
        compiler_params=pltpu.CompilerParams(collective_id=0, has_side_effects=True, vmem_limit_bytes=56 << 20),
        cost_estimate=pl.CostEstimate(flops=10 ** 10, bytes_accessed=6 * width * width, transcendentals=0),
        name="attention",
    )(tok, txt, w_qkv, b_qkv, norm128, cos_t, sin_t)


def solution(mesh):
    cp_size = mesh.shape['cp']

    def device_block(video_states, text_states, time_emb, rope_angle, ada1_w, ada1_b, norm1_par, w_qkv, b_qkv, qk_norm, w_out, b_out, ada2_w, ada2_b, norm2_par, w_up, b_up, w_down, b_down):
        vid_in = video_states[0]
        txt_in = text_states[0]
        n_text = txt_in.shape[0]
        n_vid, width = vid_in.shape
        head_dim = qk_norm.shape[-1]
        me = lax.axis_index('cp')
        txt_share = -(-n_text // (16 * cp_size)) * 16
        txt_pad = jnp.pad(txt_in, ((0, txt_share * cp_size - n_text), (0, 0)))

        vid_shift, vid_scale, vid_gate, txt_shift, txt_scale, txt_gate = modulation(time_emb, ada1_w, ada1_b)
        tok_vid = ada_norm(vid_in, norm1_par, vid_shift, vid_scale)
        tok_txt = ada_norm(txt_pad, norm1_par, txt_shift, txt_scale)
        norm128 = jnp.concatenate([qk_norm, qk_norm], axis=1)
        cos_t = jnp.tile(jnp.repeat(jnp.cos(rope_angle), 2, axis=1), (1, 2))
        sin_h = jnp.sin(rope_angle)
        sin_t = jnp.tile(jnp.stack([-sin_h, sin_h], axis=-1).reshape(n_vid, head_dim), (1, 2))
        b_row = b_qkv[None]

        att = attention(tok_vid, tok_txt, w_qkv, b_row, norm128, cos_t, sin_t, cp_size, n_text, head_dim)

        proj = jnp.dot(att, w_out, preferred_element_type=F32) + b_out
        txt_loc = lax.dynamic_slice_in_dim(txt_pad, me * txt_share, txt_share, 0)
        is_vid = lax.broadcasted_iota(jnp.int32, (n_vid + txt_share, 1), 0) < n_vid

        def by_row(vid_row, txt_row):
            return jnp.where(is_vid, vid_row, txt_row)

        x_in = jnp.concatenate([vid_in, txt_loc], axis=0).astype(F32)
        mid = (x_in + by_row(vid_gate, txt_gate) * proj).astype(BF16)
        vid_shift, vid_scale, vid_gate2, txt_shift, txt_scale, txt_gate2 = modulation(time_emb, ada2_w, ada2_b)
        tokens = ada_norm(mid, norm2_par, by_row(vid_shift, txt_shift), by_row(vid_scale, txt_scale))
        up_proj = jnp.dot(tokens, w_up, preferred_element_type=F32) + b_up
        gelu_out = jax.nn.gelu(up_proj, approximate=True).astype(BF16)
        ffn_out = jnp.dot(gelu_out, w_down, preferred_element_type=F32) + b_down
        out = (mid.astype(F32) + by_row(vid_gate2, txt_gate2) * ffn_out).astype(BF16)
        txt_out = lax.all_gather(out[n_vid:], 'cp', axis=0, tiled=True)[:n_text]
        return out[None, :n_vid], txt_out[None]

    in_specs = (P('cfg', 'cp', None), P('cfg', None, None), P('cfg', None), P('cp', None)) + (P(),) * 15
    out_specs = (P('cfg', 'cp', None), P('cfg', None, None))
    return jax.shard_map(device_block, mesh=mesh, in_specs=in_specs, out_specs=out_specs, check_vma=False)
```

time: 723 us -> 193 us (0.27)
  the two profiles are of different devices: /device:TPU:30 before, /device:TPU:21 now
where the time goes in v2:
time: 193 us
  Pallas kernels  92.1 us (48%)
  blocking collectives  48.6 us (25%)
  matrix products  41.2 us (21%)
  other arithmetic  5.27 us (3%)
  local copies, waits for them, and re-layouts  4.98 us (3%)
    pallas_call x1, Pallas kernels, attention(): pl.pallas_call(functools.partial(attention_kernel, size, n_groups, n_text...  92.1 us
    all_gather x1, blocking collectives, device_block(): txt_out = lax.all_gather(out[n_vid:], 'cp', axis=0, tiled=True)[:n_text]  48.6 us
    dot_general x1, matrix products, device_block(): ffn_out = jnp.dot(gelu_out, w_down, preferred_element_type=F32) + b_down  23.6 us
    dot_general x2, matrix products, modulation(): emb_all = jnp.dot(silu_in, ada_w, preferred_element_type=F32) + ada_b  12.1 us
    dot_general x1, matrix products, device_block(): proj = jnp.dot(att, w_out, preferred_element_type=F32) + b_out  5.49 us

profile of v2, /device:TPU:21, one launch (start us, length us, event | category | flops | bytes accessed | tf_op | source)
XLA Modules:
  0.0 193.2 jit_solution(8602116329240839300)
XLA Ops:
  0.7 6.1 %convolution_reduce_fusion.1 = f32[11520]{0:T(1024)S(1)} fusion(bf16[512,11520]{1,0:T(8,128)(2,1)} %param.23, f32[1,512]{1,0:T(1,128)} %param.21), kind=kOutput, calls=%fused_computation.48 | convolution fusion | flops 11799040 | bytes 11844608 | tf_op jit(solution)/shard_map/dot_general | solution.py:27
  6.8 0.2 slice_reduce_fusion.9
  7.0 0.2 convert_reduce_fusion
  7.2 0.4 fusion.24
  7.6 1.6 fusion.29.txt_ref
  9.2 0.2 convert_reduce_fusion.1
  9.4 0.3 fusion.32
  9.8 1.4 fusion.37.tok_ref
  11.2 0.1 fusion.69
  11.3 0.1 copy.22
  11.5 0.7 copy.24.sin_ref
  12.3 0.7 copy.23.cos_ref
  13.0 0.6 broadcast_in_dim.113.b_ref
  13.7 0.7 pad_maximum_fusion.1.norm_ref
  14.3 92.1 %attention.1 = bf16[208,1920]{1,0:T(8,128)(2,1)} custom-call(bf16[192,1920]{1,0:T(8,128)(2,1)} %fusion.37.tok_ref, bf16[256,1920]{1,0:T(8,128)(2,1)} %fusion.29.txt_ref, bf16[1920,5760]{1,0:T(8,128)(2,1)} %w_ref.1, f32[1,5760]{1,0:T(1,128)} %broadcast_in_dim.113.b_ref, f32[4,128]{1,0:T(4,128)} %pad_maximum_fusion.1.norm_ref, f32[192,128]{1,0:T(8,128)} %copy.23.cos_ref, ...), custom_call_target="tpu_custom_call" | custom-call | flops 10000000000 | bytes 22118400 | tf_op jit(solution)/shard_map/attention/pallas_call | solution.py:319
  106.5 5.5 %fusion.70 = (f32[208]{0:T(256)S(1)}, f32[208,1920]{1,0:T(8,128)S(1)}) fusion(f32[1920]{0:T(1024)S(1)} %copy-done.11, bf16[208,1920]{1,0:T(8,128)(2,1)} %attention.1, bf16[1920,1920]{1,0:T(8,128)(2,1)} %param.29, f32[1920]{0:T(1024)S(1)} %get-tuple-element.13, f32[1920]{0:T(1024)S(1)} %get-tuple-element.8, pred[208]{0:T(512)(128)(4,1)S(1)} %iota_compare_fusion, ...), kind=kOutput, calls=%fused_computation.100 | convolution fusion | flops 1537935104 | bytes 10591760 | tf_op jit(solution)/shard_map/dot_general | solution.py:368
  112.0 0.3 multiply_reduce_fusion
  112.3 0.4 copy-done.6
  112.7 6.0 %convolution_reduce_fusion = f32[11520]{0:T(1024)S(1)} fusion(bf16[512,11520]{1,0:T(8,128)(2,1)} %param.31, f32[1,512]{1,0:T(1,128)S(1)} %copy-done.6), kind=kOutput, calls=%fused_computation.47 | convolution fusion | flops 11799040 | bytes 11844608 | tf_op jit(solution)/shard_map/dot_general | solution.py:27
  118.8 0.2 slice_reduce_fusion.5
  119.0 23.6 %fusion.21 = bf16[208,1920]{1,0:T(8,128)(2,1)S(1)} fusion(f32[208,1920]{1,0:T(8,128)S(1)} %get-tuple-element.21, bf16[7680,1920]{1,0:T(8,128)(2,1)} %param.36, bf16[1920,7680]{1,0:T(8,128)(2,1)} %param.34, f32[7680]{0:T(1024)S(1)} %copy-done.10, f32[1920]{0:T(1024)S(1)} %copy-done.12, f32[1920]{0:T(1024)S(1)} %get-tuple-element.3, ...), kind=kOutput, calls=%fused_computation.24 | convolution fusion | flops 12290304000 | bytes 61480272 | tf_op jit(solution)/shard_map/dot_general | solution.py:381
  142.6 48.6 %all_gather.3 = bf16[256,1920]{1,0:T(8,128)(2,1)S(1)} all-gather(bf16[16,1920]{1,0:T(8,128)(2,1)S(1)} %slice.31), channel_id=1, replica_groups=mesh['cfg'=4,'cp'=16] {'cp'}, dimensions={0}, use_global_device_ids=true | all-gather | bytes 1044480 | tf_op jit(solution)/shard_map/all_gather | solution.py:383
  191.3 1.0 slice_bitcast_fusion
  192.3 0.9 slice_bitcast_fusion.1
  (45 shorter events, 0.4 us)
Async XLA Ops:
  0.6 6.1 %copy-start.2 = (f32[11520]{0:T(1024)S(1)}, f32[11520]{0:T(1024)}, u32[]{:S(2)}) copy-start(f32[11520]{0:T(1024)} %param.24) | copy-start | bytes 138244
  0.6 6.2 %copy-start.7 = (f32[2,1920]{1,0:T(2,128)S(1)}, f32[2,1920]{1,0:T(2,128)}, u32[]{:S(2)}) copy-start(f32[2,1920]{1,0:T(2,128)} %param.25) | copy-start | bytes 46084
  0.7 6.4 %copy-start = (bf16[1,226,1920]{2,1,0:T(8,128)(2,1)S(1)}, bf16[1,226,1920]{2,1,0:T(8,128)(2,1)}, u32[]{:S(2)}) copy-start(bf16[1,226,1920]{2,1,0:T(8,128)(2,1)} %param.20) | copy-start | bytes 2603524
  7.2 2.0 %copy-start.1 = (bf16[1,192,1920]{2,1,0:T(8,128)(2,1)S(1)}, bf16[1,192,1920]{2,1,0:T(8,128)(2,1)}, u32[]{:S(2)}) copy-start(bf16[1,192,1920]{2,1,0:T(8,128)(2,1)} %param.19) | copy-start | bytes 2211844
  9.2 1.9 %copy-start.4 = (f32[192,32]{0,1:T(8,128)S(1)}, f32[192,32]{0,1:T(8,128)}, u32[]{:S(2)}) copy-start(f32[192,32]{0,1:T(8,128)} %param.22) | copy-start | bytes 73732
  9.8 3.3 %copy-start.5 = (f32[5760]{0:T(1024)S(1)}, f32[5760]{0:T(1024)}, u32[]{:S(2)}) copy-start(f32[5760]{0:T(1024)} %param.27) | copy-start | bytes 69124
  9.8 3.9 %copy-start.9 = (f32[4,64]{1,0:T(4,128)S(1)}, f32[4,64]{1,0:T(4,128)}, u32[]{:S(2)}) copy-start(f32[4,64]{1,0:T(4,128)} %param.28) | copy-start | bytes 3076
  14.3 92.1 %copy-start.11 = (f32[1920]{0:T(1024)S(1)}, f32[1920]{0:T(1024)}, u32[]{:S(2)}) copy-start(f32[1920]{0:T(1024)} %param.30) | copy-start | bytes 23044
  112.0 0.7 copy-start.6
  112.7 6.0 %copy-start.3 = (f32[11520]{0:T(1024)S(1)}, f32[11520]{0:T(1024)}, u32[]{:S(2)}) copy-start(f32[11520]{0:T(1024)} %param.32) | copy-start | bytes 138244
  112.7 6.1 %copy-start.8 = (f32[2,1920]{1,0:T(2,128)S(1)}, f32[2,1920]{1,0:T(2,128)}, u32[]{:S(2)}) copy-start(f32[2,1920]{1,0:T(2,128)} %param.33) | copy-start | bytes 46084
  112.7 6.3 %copy-start.10 = (f32[7680]{0:T(1024)S(1)}, f32[7680]{0:T(1024)}, u32[]{:S(2)}) copy-start(f32[7680]{0:T(1024)} %param.35) | copy-start | bytes 92164
  112.7 6.3 %copy-start.12 = (f32[1920]{0:T(1024)S(1)}, f32[1920]{0:T(1024)}, u32[]{:S(2)}) copy-start(f32[1920]{0:T(1024)} %param.37) | copy-start | bytes 23044
